TPU v7x, 32 devices: a whole 2x2x4 slice. The times are simulated.
32 devices in a mesh: dp: 8 (over z, y), tensor: 4 (over x, core).
Axes of the slice: x: 2, y: 2, z: 4, core: 2. Of those that a mesh axis runs over, the one named last changes fastest.
Arguments:
- layer_input: bfloat16 [1024, 2048], P('dp'), may hold values from -6 to 6
- cotangent: bfloat16 [1024, 2048], P('dp'), may hold values from -6 to 6
- segment_ids: int32 [8, 128], P('dp'), may hold values from 0 to 3, never falling along the last dimension, each value on 1 to 64 neighbouring positions
- routes: int32 [1024, 8], P('dp'), may hold values from 0 to 63, as said below
- attn_gain: float32 [2048], replicated, may hold values from 0.25 to 1.75
- w_query: bfloat16 [2048, 4096], P(None, 'tensor'), may hold values from -0.125 to 0.125
- w_key: bfloat16 [2048, 512], P(None, 'tensor'), may hold values from -0.125 to 0.125
- w_value: bfloat16 [2048, 512], P(None, 'tensor'), may hold values from -0.125 to 0.125
- q_gain: float32 [128], replicated, may hold values from 0.5 to 1.5
- k_gain: float32 [128], replicated, may hold values from 0.5 to 1.5
- w_out: bfloat16 [4096, 2048], P('tensor'), may hold values from -0.375 to 0.375
- ffn_gain: float32 [2048], replicated, may hold values from 0.25 to 1.75
- router: bfloat16 [2048, 64], replicated
- w_gate: bfloat16 [64, 2048, 768], P('dp', None, 'tensor'), may hold values from -0.125 to 0.125
- w_up: bfloat16 [64, 2048, 768], P('dp', None, 'tensor'), may hold values from -0.125 to 0.125
- w_down: bfloat16 [64, 768, 2048], P('dp', 'tensor'), may hold values from -1.25 to 1.25
Outputs:
- layer_out: bfloat16 [1024, 2048], P('dp')
- d_input: float32 [1024, 2048], P('dp')
- grad_attn_gain: float32 [2048], replicated
- grad_query: float32 [2048, 4096], P(None, 'tensor')
- grad_key: float32 [2048, 512], P(None, 'tensor')
- grad_value: float32 [2048, 512], P(None, 'tensor')
- grad_q_gain: float32 [128], replicated
- grad_k_gain: float32 [128], replicated
- grad_out: float32 [4096, 2048], P('tensor')
- grad_ffn_gain: float32 [2048], replicated
- grad_router: float32 [2048, 64], replicated
- grad_gate: float32 [64, 2048, 768], P('dp', None, 'tensor')
- grad_up: float32 [64, 2048, 768], P('dp', None, 'tensor')
- grad_down: float32 [64, 768, 2048], P('dp', 'tensor')
Inputs may be any that keep to these rules, and one draw needn't show every extreme that they name: `segment_ids`: in each batch the numbers never fall; each of the 4 sequences has 1 to 64 tokens and one has exactly 64. `routes`: each row names 8 different experts. Among the 128 tokens of one batch no expert is named more than 40 times; in every batch several experts are named exactly 40 times, and some expert is named exactly 40 times in every batch.
All inputs are finite; a program needn't handle non-finite values.
Results may differ from a plain program's by a relative error of at most 0.018.
Values may be sent and summed in bfloat16 or wider, within the bound.
A program may use at most 320 MiB of HBM per device.

v0:
```python
import jax
import jax.numpy as jnp
from jax import lax
from jax.sharding import PartitionSpec as P

CAP = 40


EPSILON = 1e-06
ROPE_BASE = 1000000.0


def rms_scale(values, gain_vec):
    return (
        values * lax.rsqrt(jnp.mean(values * values, axis=-1, keepdims=True) + EPSILON) * gain_vec
    )


def seq_positions(segments):
    position_index = jnp.arange(segments.shape[0], dtype=jnp.int32)
    begins = jnp.concatenate([jnp.ones((1,), dtype=jnp.bool_), segments[1:] != segments[:-1]])
    first_index = lax.cummax(
        jnp.where(begins, position_index, jnp.zeros_like(position_index)), axis=0
    )
    return position_index - first_index


def rope_tables(positions, head_dim):
    half_dim = head_dim // 2
    exponent = jnp.arange(half_dim, dtype=jnp.float32) * (2.0 / head_dim)
    frequency = jnp.exp(-exponent * jnp.log(jnp.float32(ROPE_BASE)))
    angle_table = positions.astype(jnp.float32)[:, None] * frequency[None, :]
    angle_table = jnp.concatenate([angle_table, angle_table], axis=1)
    return (jnp.cos(angle_table), jnp.sin(angle_table))


def head_prep(raw_proj, gain_vec, cosine_table, sine_table):
    row_count = raw_proj.shape[0]
    head_dim = gain_vec.shape[0]
    split_heads = rms_scale(raw_proj.reshape(row_count, -1, head_dim), gain_vec)
    half_dim = head_dim // 2
    turned = jnp.concatenate([-split_heads[..., half_dim:], split_heads[..., :half_dim]], axis=-1)
    rotated = split_heads * cosine_table[:, None, :] + turned * sine_table[:, None, :]
    return rotated.reshape(row_count, -1)


def gate_weights(logits, routes):
    route_marks = (
        routes[:, :, None] == jnp.arange(logits.shape[1], dtype=jnp.int32)[None, None, :]
    ).astype(logits.dtype)
    chosen = jnp.sum(logits[:, None, :] * route_marks, axis=-1)
    return jax.nn.softmax(chosen, axis=-1)


def slot_tables(routes, experts_here, groups, capacity):
    row_count, top_count = routes.shape
    flat_routes = routes.reshape(-1)
    route_marks = (
        flat_routes[:, None] == jnp.arange(experts_here * groups, dtype=jnp.int32)[None, :]
    ).astype(jnp.int32)
    earlier = jnp.cumsum(route_marks, axis=0) - route_marks
    placing = jnp.sum(earlier * route_marks, axis=1)
    holder = flat_routes // experts_here
    local_id = flat_routes % experts_here
    buffer_slot = (local_id * groups + holder) * capacity + placing
    owner_slot = jnp.full(
        (experts_here * groups * capacity,), row_count * top_count, dtype=jnp.int32
    )
    owner_slot = owner_slot.at[buffer_slot].set(jnp.arange(row_count * top_count, dtype=jnp.int32))
    return (buffer_slot, owner_slot)


def masked_scores(query_block, key_heads, segments):
    block_rows = query_block.shape[0]
    scores = jnp.einsum(
        "qhgd,shd->hgqs", query_block, key_heads, preferred_element_type=jnp.float32
    )
    scores = scores * query_block.shape[-1] ** (-0.5)
    query_index = jnp.arange(block_rows, dtype=jnp.int32)
    key_index = jnp.arange(key_heads.shape[0], dtype=jnp.int32)
    allowed = (segments[:, None] == segments[None, :]) & (
        query_index[:, None] >= key_index[None, :]
    )
    return jnp.where(allowed[None, None], scores, -jnp.inf)


def attend(query_rot, key_rot, value_rot, segments, kv_count, head_dim):
    row_count = query_rot.shape[0]
    query_heads = query_rot.reshape(row_count, kv_count, -1, head_dim)
    key_heads = key_rot.reshape(row_count, kv_count, head_dim)
    value_heads = value_rot.reshape(row_count, kv_count, head_dim)
    block_rows = min(512, row_count)
    scores = masked_scores(query_heads, key_heads, segments)
    highest = jnp.max(scores, axis=-1, keepdims=True)
    exponent = jnp.exp(scores - highest)
    denominator = jnp.sum(exponent, axis=-1, keepdims=True)
    probs_bf = (exponent / denominator).astype(jnp.bfloat16)
    lse_list = highest[..., 0] + jnp.log(denominator[..., 0])
    head_mix = jnp.einsum(
        "hgqs,shd->qhgd", probs_bf, value_heads, preferred_element_type=jnp.float32
    )
    out_list = head_mix.astype(jnp.bfloat16).reshape(block_rows, -1)
    return (out_list, lse_list)


def attend_back(query_rot, key_rot, value_rot, segments, log_total, grad_heads, kv_count, head_dim):
    row_count = query_rot.shape[0]
    query_heads = query_rot.reshape(row_count, kv_count, -1, head_dim)
    key_heads = key_rot.reshape(row_count, kv_count, head_dim)
    value_heads = value_rot.reshape(row_count, kv_count, head_dim)
    block_rows = min(512, row_count)
    score_scale = head_dim ** (-0.5)
    scores = masked_scores(query_heads, key_heads, segments)
    probabilities = jnp.exp(scores - log_total[..., 0:block_rows, None])
    grad_block = grad_heads.reshape(block_rows, kv_count, -1, head_dim)
    d_values = jnp.einsum(
        "hgqs,qhgd->shd",
        probabilities.astype(jnp.bfloat16),
        grad_block,
        preferred_element_type=jnp.float32,
    )
    d_prob = jnp.einsum(
        "qhgd,shd->hgqs", grad_block, value_heads, preferred_element_type=jnp.float32
    )
    row_delta = jnp.sum(probabilities * d_prob, axis=-1, keepdims=True)
    d_score = (probabilities * (d_prob - row_delta) * score_scale).astype(jnp.bfloat16)
    dq_list = jnp.einsum(
        "hgqs,shd->qhgd", d_score, key_heads, preferred_element_type=jnp.float32
    ).reshape(block_rows, -1)
    d_keys = jnp.einsum("hgqs,qhgd->shd", d_score, query_heads, preferred_element_type=jnp.float32)
    return (dq_list, d_keys.reshape(row_count, -1), d_values.reshape(row_count, -1))


def on_device(
    layer_input,
    cotangent,
    segment_ids,
    routes,
    attn_gain,
    w_query,
    w_key,
    w_value,
    q_gain,
    k_gain,
    w_out,
    ffn_gain,
    router,
    w_gate,
    w_up,
    w_down,
):
    segments = segment_ids[0]
    row_count, model_width = layer_input.shape
    top_count = routes.shape[1]
    head_dim = q_gain.shape[0]
    kv_here = w_key.shape[1] // head_dim
    experts_here = w_gate.shape[0]
    groups = router.shape[1] // experts_here
    cosine_table, sine_table = rope_tables(seq_positions(segments), head_dim)
    x_float = layer_input.astype(jnp.float32)
    normed1 = rms_scale(x_float, attn_gain).astype(jnp.bfloat16)
    query_raw = jnp.dot(normed1, w_query, preferred_element_type=jnp.float32)
    key_raw = jnp.dot(normed1, w_key, preferred_element_type=jnp.float32)
    value_rot = jnp.dot(normed1, w_value, preferred_element_type=jnp.float32).astype(jnp.bfloat16)
    query_rot = head_prep(query_raw, q_gain, cosine_table, sine_table).astype(jnp.bfloat16)
    key_rot = head_prep(key_raw, k_gain, cosine_table, sine_table).astype(jnp.bfloat16)
    attn_mixed, log_total = attend(query_rot, key_rot, value_rot, segments, kv_here, head_dim)
    partial_attn = jnp.dot(attn_mixed, w_out, preferred_element_type=jnp.float32)
    residual = x_float + lax.psum(partial_attn, "tensor")
    normed2 = rms_scale(residual, ffn_gain).astype(jnp.bfloat16)
    logits = jnp.dot(normed2, router, preferred_element_type=jnp.float32)
    weights = gate_weights(logits, routes)
    buffer_slot, owner_slot = slot_tables(routes, experts_here, groups, CAP)
    token_of = owner_slot // top_count
    normed_pad = jnp.concatenate([normed2, jnp.zeros((1, model_width), jnp.bfloat16)], axis=0)
    outgoing = normed_pad[token_of].reshape(experts_here, groups, CAP, model_width)
    received = lax.all_to_all(outgoing, "dp", split_axis=1, concat_axis=1, tiled=True)
    expert_in = received.reshape(experts_here, groups * CAP, model_width)
    gate_pre = jnp.einsum("erd,edf->erf", expert_in, w_gate, preferred_element_type=jnp.float32)
    up_pre = jnp.einsum("erd,edf->erf", expert_in, w_up, preferred_element_type=jnp.float32)
    sigmoid_g = jax.nn.sigmoid(gate_pre)
    silu_g = gate_pre * sigmoid_g
    activation = (silu_g * up_pre).astype(jnp.bfloat16)
    expert_out = jnp.einsum(
        "erf,efd->erd", activation, w_down, preferred_element_type=jnp.float32
    ).astype(jnp.bfloat16)
    returned = lax.all_to_all(
        expert_out.reshape(experts_here, groups, CAP, model_width),
        "dp",
        split_axis=1,
        concat_axis=1,
        tiled=True,
    )
    picked = returned.reshape(-1, model_width)[buffer_slot].reshape(
        row_count, top_count, model_width
    )
    moe_part = jnp.sum(weights[:, :, None] * picked, axis=1)
    moe_total = lax.psum(moe_part, "tensor")
    layer_out = (residual + moe_total).astype(jnp.bfloat16)
    cot_float = cotangent.astype(jnp.float32)
    weight_pad = jnp.concatenate([weights.reshape(-1), jnp.zeros((1,), jnp.float32)])
    cot_pad = jnp.concatenate([cotangent, jnp.zeros((1, model_width), jnp.bfloat16)], axis=0)
    slot_grad = (weight_pad[owner_slot][:, None] * cot_pad[token_of]).astype(jnp.bfloat16)
    d_expert_out = lax.all_to_all(
        slot_grad.reshape(experts_here, groups, CAP, model_width),
        "dp",
        split_axis=1,
        concat_axis=1,
        tiled=True,
    ).reshape(experts_here, groups * CAP, model_width)
    d_act = jnp.einsum("erd,efd->erf", d_expert_out, w_down, preferred_element_type=jnp.float32)
    d_gate = (d_act * up_pre * sigmoid_g * (1.0 + gate_pre * (1.0 - sigmoid_g))).astype(
        jnp.bfloat16
    )
    d_up = (d_act * silu_g).astype(jnp.bfloat16)
    grad_down = jnp.einsum(
        "erf,erd->efd", activation, d_expert_out, preferred_element_type=jnp.float32
    )
    grad_gate = jnp.einsum("erd,erf->edf", expert_in, d_gate, preferred_element_type=jnp.float32)
    grad_up = jnp.einsum("erd,erf->edf", expert_in, d_up, preferred_element_type=jnp.float32)
    d_expert_in = jnp.einsum("erf,edf->erd", d_gate, w_gate, preferred_element_type=jnp.float32)
    d_expert_in = (
        d_expert_in + jnp.einsum("erf,edf->erd", d_up, w_up, preferred_element_type=jnp.float32)
    ).astype(jnp.bfloat16)
    d_back = lax.all_to_all(
        d_expert_in.reshape(experts_here, groups, CAP, model_width),
        "dp",
        split_axis=1,
        concat_axis=1,
        tiled=True,
    )
    d_rows = d_back.reshape(-1, model_width)[buffer_slot].reshape(row_count, top_count, model_width)
    d_norm2_part = jnp.sum(d_rows.astype(jnp.float32), axis=1)
    dw_part = jnp.sum(picked.astype(jnp.float32) * cot_float[:, None, :], axis=-1)
    d_norm2_moe, d_weights = lax.psum((d_norm2_part, dw_part), "tensor")
    gate_back = jax.vjp(lambda logit_in: gate_weights(logit_in, routes), logits)[1]
    d_logits = gate_back(d_weights)[0].astype(jnp.bfloat16)
    grad_router = jnp.dot(normed2.T, d_logits, preferred_element_type=jnp.float32)
    d_norm2 = d_norm2_moe + jnp.dot(d_logits, router.T, preferred_element_type=jnp.float32)
    norm2_back = jax.vjp(rms_scale, residual, ffn_gain)[1]
    d_resid_norm, grad_ffn_gain = norm2_back(d_norm2)
    d_resid = cot_float + d_resid_norm
    d_resid_bf = d_resid.astype(jnp.bfloat16)
    grad_out_w = jnp.dot(attn_mixed.T, d_resid_bf, preferred_element_type=jnp.float32)
    d_attn = jnp.dot(d_resid_bf, w_out.T, preferred_element_type=jnp.float32).astype(jnp.bfloat16)
    d_qrot, d_krot, d_vals = attend_back(
        query_rot, key_rot, value_rot, segments, log_total, d_attn, kv_here, head_dim
    )
    q_back = jax.vjp(
        lambda raw_in, gain_in: head_prep(raw_in, gain_in, cosine_table, sine_table),
        query_raw,
        q_gain,
    )[1]
    d_qraw, grad_qgain = q_back(d_qrot)
    k_back = jax.vjp(
        lambda raw_in, gain_in: head_prep(raw_in, gain_in, cosine_table, sine_table),
        key_raw,
        k_gain,
    )[1]
    d_kraw, grad_kgain = k_back(d_krot)
    dq_bf = d_qraw.astype(jnp.bfloat16)
    dk_bf = d_kraw.astype(jnp.bfloat16)
    dv_bf = d_vals.astype(jnp.bfloat16)
    grad_query = jnp.dot(normed1.T, dq_bf, preferred_element_type=jnp.float32)
    grad_key = jnp.dot(normed1.T, dk_bf, preferred_element_type=jnp.float32)
    grad_value = jnp.dot(normed1.T, dv_bf, preferred_element_type=jnp.float32)
    d_norm1_part = jnp.dot(dq_bf, w_query.T, preferred_element_type=jnp.float32)
    d_norm1_part = d_norm1_part + jnp.dot(dk_bf, w_key.T, preferred_element_type=jnp.float32)
    d_norm1_part = d_norm1_part + jnp.dot(dv_bf, w_value.T, preferred_element_type=jnp.float32)
    d_norm1, grad_qgain, grad_kgain = lax.psum((d_norm1_part, grad_qgain, grad_kgain), "tensor")
    norm1_back = jax.vjp(rms_scale, x_float, attn_gain)[1]
    d_x_norm, grad_attn_gain = norm1_back(d_norm1)
    d_input = d_resid + d_x_norm
    (
        grad_query,
        grad_key,
        grad_value,
        grad_out_w,
        grad_router,
        grad_attn_gain,
        grad_ffn_gain,
        grad_qgain,
        grad_kgain,
    ) = lax.psum(
        (
            grad_query,
            grad_key,
            grad_value,
            grad_out_w,
            grad_router,
            grad_attn_gain,
            grad_ffn_gain,
            grad_qgain,
            grad_kgain,
        ),
        "dp",
    )
    return (
        layer_out,
        d_input,
        grad_attn_gain,
        grad_query,
        grad_key,
        grad_value,
        grad_qgain,
        grad_kgain,
        grad_out_w,
        grad_ffn_gain,
        grad_router,
        grad_gate,
        grad_up,
        grad_down,
    )


def solution(mesh):
    in_specs = (
        P("dp", None),
        P("dp", None),
        P("dp", None),
        P("dp", None),
        P(),
        P(None, "tensor"),
        P(None, "tensor"),
        P(None, "tensor"),
        P(),
        P(),
        P("tensor", None),
        P(),
        P(),
        P("dp", None, "tensor"),
        P("dp", None, "tensor"),
        P("dp", "tensor", None),
    )
    out_specs = (
        P("dp", None),
        P("dp", None),
        P(),
        P(None, "tensor"),
        P(None, "tensor"),
        P(None, "tensor"),
        P(),
        P(),
        P("tensor", None),
        P(),
        P(),
        P("dp", None, "tensor"),
        P("dp", None, "tensor"),
        P("dp", "tensor", None),
    )
    return jax.shard_map(
        on_device, mesh=mesh, in_specs=in_specs, out_specs=out_specs, check_vma=False
    )
```

profile of v0, /device:TPU:0, one launch (start us, length us, event | category | flops | bytes accessed | tf_op | source)
XLA Modules:
  0.0 1818.1 jit_solution(2075278266386348362)
XLA Ops:
  8.6 3.1 fusion.73
  25.2 18.0 reduce-window.19
  44.0 4.3 scatter_custom_fusion
  48.3 15.8 all-reduce.15.cloned.1.call-done
  66.8 10.7 gather_fusion
  77.5 10.3 copy.260
  87.7 5.6 all-to-all-start
  93.5 10.7 gather_fusion.3
  104.7 13.6 gather_fusion.2
  118.5 10.5 fusion
  128.9 192.0 %all-to-all-done = bf16[8,8,40,2048]{3,2,0,1:T(8,128)(2,1)} async-done(((bf16[8,8,40,2048]{3,2,0,1:T(8,128)(2,1)}), bf16[8,8,40,2048]{3,2,0,1:T(8,128)(2,1)}, u32[]{:S(2)}, u32[]{:S(2)}) %all-to-all-start) | async-done | bytes 10485792 | tf_op jit(solution)/shard_map/all_to_all | solution.py:177
  321.0 5.4 all-to-all-start.2
  326.3 10.3 copy.261
  336.6 11.4 fusion.84
  348.0 11.4 fusion.85
  359.3 193.5 %all-to-all-done.2 = bf16[8,8,40,2048]{3,2,0,1:T(8,128)(2,1)} async-done(((bf16[8,8,40,2048]{3,2,0,1:T(8,128)(2,1)}), bf16[8,8,40,2048]{3,2,0,1:T(8,128)(2,1)}, u32[]{:S(2)}, u32[]{:S(2)}) %all-to-all-start.2) | async-done | bytes 10485792 | tf_op jit(solution)/shard_map/all_to_all | solution.py:204
  552.9 10.3 copy.267
  563.2 13.6 multiply_convert_fusion
  576.7 10.2 convolution_convert_fusion
  586.9 10.0 copy.262
  597.0 5.3 all-to-all-start.1
  602.3 12.7 fusion.86
  615.0 15.0 add_convert_fusion
  630.0 10.2 copy.268
  640.2 189.2 %all-to-all-done.1 = bf16[8,8,40,2048]{3,2,0,1:T(8,128)(2,1)} async-done(((bf16[8,8,40,2048]{3,2,0,1:T(8,128)(2,1)}), bf16[8,8,40,2048]{3,2,0,1:T(8,128)(2,1)}, u32[]{:S(2)}, u32[]{:S(2)}) %all-to-all-start.1) | async-done | bytes 10485792 | tf_op jit(solution)/shard_map/all_to_all | solution.py:187
  829.4 5.1 all-to-all-start.3
  835.7 10.3 copy.263
  845.9 14.1 gather_fusion.1
  860.1 5.8 fusion.2
  866.0 6.2 psum.115
  872.3 189.5 %all-to-all-done.3 = bf16[8,8,40,2048]{3,2,0,1:T(8,128)(2,1)} async-done(((bf16[8,8,40,2048]{3,2,0,1:T(8,128)(2,1)}), bf16[8,8,40,2048]{3,2,0,1:T(8,128)(2,1)}, u32[]{:S(2)}, u32[]{:S(2)}) %all-to-all-start.3) | async-done | bytes 10485792 | tf_op jit(solution)/shard_map/all_to_all | solution.py:225
  1061.8 10.3 copy.269
  1072.1 14.1 gather_fusion.4
  1086.2 6.1 convert_reduce_fusion
  1093.7 34.3 %all-reduce.17.cloned.1.call-done = f32[128,2048]{1,0:T(8,128)} async-done(((f32[128,2048]{1,0:T(8,128)}), f32[128,2048]{1,0:T(8,128)}) %all-reduce.17.cloned.1.call-update) | async-done | bytes 1048592 | tf_op jit(solution)/shard_map/psum | solution.py:235
  1128.1 2.5 multiply_reduce_fusion
  1136.9 2.7 multiply_reduce_fusion.3
  1156.6 4.7 fusion.71
  1161.4 4.6 fusion.30
  1166.0 12.8 fusion.88
  1178.9 12.5 fusion.89
  1191.5 6.6 fusion.90
  1198.1 6.7 all-reduce.8
  1208.6 39.5 %all-reduce.6 = (f32[2048]{0:T(1024)}, f32[128]{0:T(128)}, f32[128]{0:T(128)}, f32[2048]{0:T(1024)}) all-reduce(f32[2048]{0:T(1024)S(1)} %get-tuple-element.18, f32[128]{0:T(128)S(1)} %get-tuple-element.33, f32[128]{0:T(128)S(1)} %get-tuple-element.34, f32[2048]{0:T(1024)S(1)} %copy-done.50), channel_id=1, replica_groups=mesh['dp'=8,'tensor'=4] {'dp'}, use_global_device_ids=true, to_apply=%region_30.31 | all-reduce | flops 4352 | bytes 34816 | tf_op jit(solution)/shard_map/psum | solution.py:284
  1250.2 2.5 fusion.14
  1252.7 543.6 %all-reduce.19.cloned.1.call-done = (f32[2048,1024]{1,0:T(8,128)}, f32[2048,128]{1,0:T(8,128)}, f32[2048,128]{1,0:T(8,128)}, f32[1024,2048]{1,0:T(8,128)}, f32[2048,64]{0,1:T(8,128)}) async-done(((f32[2048,1024]{1,0:T(8,128)}, f32[2048,128]{1,0:T(8,128)}, f32[2048,128]{1,0:T(8,128)}, f32[1024,2048]{1,0:T(8,128)}, f32[2048,64]{0,1:T(8,128)}), (f32[2048,1024]{1,0:T(8,128)}, f32[2048,128]{1,0:T(8,128)}, ...) | async-done | bytes 19398672 | tf_op jit(solution)/shard_map/psum | solution.py:284
  1796.3 8.6 copy.317
  1806.9 3.4 copy.320
  (271 shorter events, 52.9 us)
Async XLA Ops:
  7.3 56.9 %all-reduce.15.cloned.1.call-start = ((), (), s32[]{:S(2)}) async-start(), calls=%async_computation.4 | async-start | bytes 2097152 | tf_op jit(solution)/shard_map/psum | solution.py:169
  8.6 9.5 copy-start.53
  12.3 8.7 copy-start.10
  14.0 7.5 copy-start.42
  15.1 9.6 copy-start.30
  15.1 9.6 copy-start.38
  21.1 22.8 %copy-start.19 = (bf16[128,1024]{1,0:T(8,128)(2,1)}, bf16[128,1024]{1,0:T(8,128)(2,1)S(1)}, u32[]{:S(2)}) copy-start(bf16[128,1024]{1,0:T(8,128)(2,1)S(1)} %add_convert_fusion.2) | copy-start | bytes 786436
  23.0 43.6 %copy-start.44 = (f32[2048]{0:T(1024)S(1)}, f32[2048]{0:T(1024)}, u32[]{:S(2)}) copy-start(f32[2048]{0:T(1024)} %param.27) | copy-start | bytes 24580
  43.9 33.5 %copy-start.57 = (s32[1024,1]{0,1:T(1,128)}, s32[1024,1]{0,1:T(1,128)S(1)}, u32[]{:S(2)}) copy-start(s32[1024,1]{0,1:T(1,128)S(1)} %compare_select_fusion.1) | copy-start | bytes 12292
  65.6 11.8 copy-start.64
  87.7 233.2 %all-to-all-start = ((bf16[8,8,40,2048]{3,2,0,1:T(8,128)(2,1)}), bf16[8,8,40,2048]{3,2,0,1:T(8,128)(2,1)}, u32[]{:S(2)}, u32[]{:S(2)}) async-start(bf16[8,8,40,2048]{3,2,0,1:T(8,128)(2,1)} %copy.260), calls=%async_computation | async-start | bytes 20971520 | tf_op jit(solution)/shard_map/all_to_all | solution.py:177
  93.4 10.7 copy-start.25
  321.0 231.9 %all-to-all-start.2 = ((bf16[8,8,40,2048]{3,2,0,1:T(8,128)(2,1)}), bf16[8,8,40,2048]{3,2,0,1:T(8,128)(2,1)}, u32[]{:S(2)}, u32[]{:S(2)}) async-start(bf16[8,8,40,2048]{3,2,0,1:T(8,128)(2,1)} %fusion), calls=%async_computation.2 | async-start | bytes 20971520 | tf_op jit(solution)/shard_map/all_to_all | solution.py:204
  576.7 10.2 copy-start.8
  597.0 232.4 %all-to-all-start.1 = ((bf16[8,8,40,2048]{3,2,0,1:T(8,128)(2,1)}), bf16[8,8,40,2048]{3,2,0,1:T(8,128)(2,1)}, u32[]{:S(2)}, u32[]{:S(2)}) async-start(bf16[8,8,40,2048]{3,2,0,1:T(8,128)(2,1)} %copy.262), calls=%async_computation.1 | async-start | bytes 20971520 | tf_op jit(solution)/shard_map/all_to_all | solution.py:187
  640.2 194.7 %copy-start.20 = (bf16[128,1024]{1,0:T(8,128)(2,1)S(1)}, bf16[128,1024]{1,0:T(8,128)(2,1)}, u32[]{:S(2)}) copy-start(bf16[128,1024]{1,0:T(8,128)(2,1)} %copy-done.19) | copy-start | bytes 786436
  640.2 195.4 %copy-start.58 = (s32[1024,1]{0,1:T(1,128)S(1)}, s32[1024,1]{0,1:T(1,128)}, u32[]{:S(2)}) copy-start(s32[1024,1]{0,1:T(1,128)} %copy-done.57) | copy-start | bytes 12292
  640.2 195.4 %copy-start.47 = (f32[8,128]{1,0:T(8,128)S(1)}, f32[8,128]{1,0:T(8,128)}, u32[]{:S(2)}) copy-start(f32[8,128]{1,0:T(8,128)} %copy-done.46) | copy-start | bytes 12292
  640.2 195.4 %copy-start.56 = (f32[8,128]{1,0:T(8,128)S(1)}, f32[8,128]{1,0:T(8,128)}, u32[]{:S(2)}) copy-start(f32[8,128]{1,0:T(8,128)} %copy-done.55) | copy-start | bytes 12292
  829.4 232.4 %all-to-all-start.3 = ((bf16[8,8,40,2048]{3,2,0,1:T(8,128)(2,1)}), bf16[8,8,40,2048]{3,2,0,1:T(8,128)(2,1)}, u32[]{:S(2)}, u32[]{:S(2)}) async-start(bf16[8,8,40,2048]{3,2,0,1:T(8,128)(2,1)} %copy.268), calls=%async_computation.3 | async-start | bytes 20971520 | tf_op jit(solution)/shard_map/all_to_all | solution.py:225
  834.5 293.5 %all-reduce.17.cloned.1.call-start = ((), (), s32[]{:S(2)}) async-start(), calls=%async_computation.5 | async-start | bytes 2097152 | tf_op jit(solution)/shard_map/psum | solution.py:235
  1086.2 41.9 %copy-start.4 = (f32[128,2048]{1,0:T(8,128)S(1)}, f32[128,2048]{1,0:T(8,128)}, u32[]{:S(2)}) copy-start(f32[128,2048]{1,0:T(8,128)} %copy-done.3) | copy-start | bytes 3145732
  1086.2 41.9 %copy-start.45 = (f32[2048]{0:T(1024)S(1)}, f32[2048]{0:T(1024)}, u32[]{:S(2)}) copy-start(f32[2048]{0:T(1024)} %param.27) | copy-start | bytes 24580
  1086.2 41.9 %copy-start.65 = (f32[128]{0:T(128)S(1)}, f32[128]{0:T(128)}, u32[]{:S(2)}) copy-start(f32[128]{0:T(128)} %copy-done.64) | copy-start | bytes 1540
  1086.2 44.4 %copy-start.71 = (f32[128]{0:T(128)S(1)}, f32[128]{0:T(128)}, u32[]{:S(2)}) copy-start(f32[128]{0:T(128)} %copy-done.70) | copy-start | bytes 1540
  1086.2 44.4 %copy-start.18 = (bf16[128,2048]{1,0:T(8,128)(2,1)S(1)}, bf16[128,2048]{1,0:T(8,128)(2,1)}, u32[]{:S(2)}) copy-start(bf16[128,2048]{1,0:T(8,128)(2,1)} %param.17) | copy-start | bytes 1572868
  1092.3 114.6 %all-reduce.21.cloned.1.call-start = ((), (), s32[]{:S(2)}) async-start(), calls=%async_computation.7 | async-start | bytes 4194304 | tf_op jit(solution)/shard_map/psum | solution.py:198
  1132.6 12.4 copy-start.2
  1132.6 12.4 copy-start.35
  1136.9 11.6 copy-start.29
  1139.6 7.5 copy-start.40
  1139.6 8.9 copy-start.41
  1142.1 8.6 copy-start.11
  1142.1 8.6 copy-start.22
  1142.1 9.4 copy-start.7
  1145.0 8.1 copy-start.60
  1145.0 8.1 copy-start.62
  1154.9 641.4 %all-reduce.19.cloned.1.call-start = ((), (), s32[]{:S(2)}) async-start(), calls=%async_computation.6 | async-start | bytes 38797312 | tf_op jit(solution)/shard_map/psum | solution.py:284
  1166.0 12.9 copy-start.15
  1166.0 25.4 %slice-start = ((s8[10485760]{0:T(1024)(128)(4,1)}), s8[4194304]{0:T(1024)(128)(4,1)S(1)}, s32[]{:S(2)}) async-start(s8[10485760]{0:T(1024)(128)(4,1)} %bitcast.196), calls=%async_computation.8 | async-start | bytes 8388608
  1166.0 25.4 %slice-start.1 = ((s8[10485760]{0:T(1024)(128)(4,1)}), s8[4194304]{0:T(1024)(128)(4,1)S(1)}, s32[]{:S(2)}) async-start(s8[10485760]{0:T(1024)(128)(4,1)} %bitcast.196), calls=%async_computation.9 | async-start | bytes 8388608
  1178.9 12.5 slice-start.2
  1178.9 12.5 copy-start.16
  1191.4 17.2 copy-start.50
  1191.5 56.6 %copy-start.68 = (f32[128]{0:T(128)S(1)}, f32[128]{0:T(128)}, u32[]{:S(2)}) copy-start(f32[128]{0:T(128)} %copy-done.67) | copy-start | bytes 1540
  1796.3 8.6 copy-start.27
  1796.3 9.6 copy-start.26
  1796.3 10.5 copy-start.9
  (37 other events, 143.3 us)
Sparse Core Ops, SparseCore 0:
  24.9 39.2 all-reduce.14
  1092.5 35.5 all-reduce.16
  1155.0 51.9 all-reduce.20
  1213.1 583.1 all-reduce.18
where the time goes:
time: 1830 us; the launch traced here: 1820 us
  waiting for transfers between devices  1360 us (74%)
  local copies, waits for them, and re-layouts  166 us (9%)
  matrix products  139 us (8%)
  other arithmetic  62.4 us (3%)
  blocking collectives  52.4 us (3%)
  starting transfers between devices  22.3 us (1%)
    psum x1, waiting for transfers between devices, on_device(): lax.psum((grad_query, grad_key, grad_value, grad_out_w, grad_router, grad...  544 us
    all_to_all x1, waiting for transfers between devices, on_device(): lax.all_to_all(slot_grad.reshape(experts_here, groups, CAP, model_width),...  194 us
    all_to_all x1, waiting for transfers between devices, on_device(): lax.all_to_all(outgoing, 'dp', split_axis=1, concat_axis=1, tiled=True)  192 us
    all_to_all x1, waiting for transfers between devices, on_device(): lax.all_to_all(d_expert_in.reshape(experts_here, groups, CAP, model_width...  190 us
    all_to_all x1, waiting for transfers between devices, on_device(): lax.all_to_all(expert_out.reshape(experts_here, groups, CAP, model_width)...  189 us
    psum x1, blocking collectives, on_device(): lax.psum((grad_query, grad_key, grad_value, grad_out_w, grad_router, grad...  39.5 us
  transfers between devices with their start and end apart: 8, of which 8 were waited for; matrix products, arithmetic and copies ran while one was open for 12% of the time, Pallas kernels for 0%

commit v1 on v0

v1 whole, which is shorter than its diff:
```python
import jax
import jax.numpy as jnp
from jax import lax
from jax.sharding import PartitionSpec as P

CAP = 40
EPSILON = 1e-06
ROPE_BASE = 1000000.0
BF = jnp.bfloat16
F32 = jnp.float32


def rms_scale(values, gain_vec):
    return (
        values * lax.rsqrt(jnp.mean(values * values, axis=-1, keepdims=True) + EPSILON) * gain_vec
    )


def seq_positions(segments):
    index = jnp.arange(segments.shape[0], dtype=jnp.int32)
    before = jnp.sum((segments[None, :] < segments[:, None]).astype(jnp.int32), axis=1)
    return index - before


def rope_tables(positions, head_dim):
    half_dim = head_dim // 2
    exponent = jnp.arange(half_dim, dtype=F32) * (2.0 / head_dim)
    frequency = jnp.exp(-exponent * jnp.log(F32(ROPE_BASE)))
    angle_table = positions.astype(F32)[:, None] * frequency[None, :]
    angle_table = jnp.concatenate([angle_table, angle_table], axis=1)
    return (jnp.cos(angle_table), jnp.sin(angle_table))


def head_prep(raw_proj, gain_vec, cosine_table, sine_table):
    row_count = raw_proj.shape[0]
    head_dim = gain_vec.shape[0]
    split_heads = rms_scale(raw_proj.reshape(row_count, -1, head_dim), gain_vec)
    half_dim = head_dim // 2
    turned = jnp.concatenate([-split_heads[..., half_dim:], split_heads[..., :half_dim]], axis=-1)
    rotated = split_heads * cosine_table[:, None, :] + turned * sine_table[:, None, :]
    return rotated.reshape(row_count, -1)


def masked_scores(query_heads, key_heads, segments):
    rows = query_heads.shape[0]
    scores = jnp.einsum("qhgd,shd->hgqs", query_heads, key_heads, preferred_element_type=F32)
    scores = scores * query_heads.shape[-1] ** (-0.5)
    index = jnp.arange(rows, dtype=jnp.int32)
    allowed = (segments[:, None] == segments[None, :]) & (index[:, None] >= index[None, :])
    return jnp.where(allowed[None, None], scores, -jnp.inf)


def attend(query_rot, key_rot, value_rot, segments, kv_count, head_dim):
    rows = query_rot.shape[0]
    query_heads = query_rot.reshape(rows, kv_count, -1, head_dim)
    key_heads = key_rot.reshape(rows, kv_count, head_dim)
    value_heads = value_rot.reshape(rows, kv_count, head_dim)
    scores = masked_scores(query_heads, key_heads, segments)
    highest = jnp.max(scores, axis=-1, keepdims=True)
    exponent = jnp.exp(scores - highest)
    denominator = jnp.sum(exponent, axis=-1, keepdims=True)
    probs_bf = (exponent / denominator).astype(BF)
    lse = highest[..., 0] + jnp.log(denominator[..., 0])
    mixed = jnp.einsum("hgqs,shd->qhgd", probs_bf, value_heads, preferred_element_type=F32)
    return (mixed.astype(BF).reshape(rows, -1), lse)


def attend_back(query_rot, key_rot, value_rot, segments, lse, grad_heads, kv_count, head_dim):
    rows = query_rot.shape[0]
    query_heads = query_rot.reshape(rows, kv_count, -1, head_dim)
    key_heads = key_rot.reshape(rows, kv_count, head_dim)
    value_heads = value_rot.reshape(rows, kv_count, head_dim)
    scores = masked_scores(query_heads, key_heads, segments)
    probs = jnp.exp(scores - lse[..., None])
    grad_block = grad_heads.reshape(rows, kv_count, -1, head_dim)
    d_values = jnp.einsum(
        "hgqs,qhgd->shd", probs.astype(BF), grad_block, preferred_element_type=F32
    )
    d_prob = jnp.einsum("qhgd,shd->hgqs", grad_block, value_heads, preferred_element_type=F32)
    row_delta = jnp.sum(probs * d_prob, axis=-1, keepdims=True)
    d_score = (probs * (d_prob - row_delta) * head_dim ** (-0.5)).astype(BF)
    d_query = jnp.einsum("hgqs,shd->qhgd", d_score, key_heads, preferred_element_type=F32)
    d_keys = jnp.einsum("hgqs,qhgd->shd", d_score, query_heads, preferred_element_type=F32)
    return (d_query.reshape(rows, -1), d_keys.reshape(rows, -1), d_values.reshape(rows, -1))


def make_device_fn(mesh):
    n_dp = mesh.shape["dp"]
    n_tp = mesh.shape["tensor"]

    def rot(x, step):
        return lax.ppermute(x, "dp", [(i, (i + step) % n_dp) for i in range(n_dp)])

    def flip(x, mask):
        return lax.ppermute(x, "tensor", [(i, i ^ mask) for i in range(n_tp)])

    def relative(quarters):
        own = lax.axis_index("tensor")
        for bit in (1, 2):
            on = (own & bit) != 0
            quarters = [
                jnp.where(on, quarters[q ^ bit], quarters[q]) for q in range(n_tp)
            ]
        return quarters

    def split_relative(x):
        return relative(jnp.split(x, n_tp, axis=0))

    def over_tensor(x):
        across = flip(x, 2)
        return [x, flip(x, 1), across, flip(across, 1)]

    def gather_tokens(x):
        blocks = []
        for step in range(n_dp):
            blocks.extend(over_tensor(x if step == 0 else rot(x, step)))
        return jnp.concatenate(blocks, axis=0)

    def gather_batches(x):
        return jnp.concatenate([x] + [rot(x, s) for s in range(1, n_dp)], axis=0)

    def add_up(a, b, kind):
        return (a.astype(F32) + b.astype(F32)).astype(kind)

    def reduce_tensor(parts, kind, last):
        low = add_up(parts[0], flip(parts[1], 1), kind)
        high = add_up(parts[2], flip(parts[3], 1), kind)
        return add_up(low, flip(high, 2), last)

    def reduce_tokens(x, rows):
        grid = x.reshape(n_dp, n_tp, rows, x.shape[1])
        total = None
        for step in list(range(1, n_dp)) + [0]:
            part = reduce_tensor([grid[step, m] for m in range(n_tp)], BF, BF)
            part = part if step == 0 else rot(part, n_dp - step)
            total = part.astype(F32) if total is None else total + part.astype(F32)
        return total

    def sum_all(x):
        total = x
        for step in range(1, n_dp):
            total = total + rot(x, step)
        return sum(over_tensor(total)[1:], total)

    def on_device(
        layer_input,
        cotangent,
        segment_ids,
        routes,
        attn_gain,
        w_query,
        w_key,
        w_value,
        q_gain,
        k_gain,
        w_out,
        ffn_gain,
        router,
        w_gate,
        w_up,
        w_down,
    ):
        segments = segment_ids[0]
        row_count, width = layer_input.shape
        own_rows = row_count // n_tp
        head_dim = q_gain.shape[0]
        kv_here = w_key.shape[1] // head_dim
        experts_here = w_gate.shape[0]
        experts = router.shape[1]
        tokens = n_dp * row_count
        slots = n_dp * CAP
        tensor_at = lax.axis_index("tensor")
        first_expert = lax.axis_index("dp") * experts_here
        first_row = tensor_at * own_rows

        def own(x):
            return lax.dynamic_slice_in_dim(x, first_row, own_rows, axis=0)

        route_rows = jnp.concatenate(split_relative(routes), axis=0)
        routes_all = gather_batches(route_rows.T.reshape(1, -1, row_count))
        routes_all = jnp.transpose(routes_all, (0, 2, 1)).reshape(tokens, -1)
        cot_all = gather_tokens(own(cotangent))

        cosine_table, sine_table = rope_tables(seq_positions(segments), head_dim)
        x_float = layer_input.astype(F32)
        normed1 = rms_scale(x_float, attn_gain).astype(BF)
        query_raw = jnp.dot(normed1, w_query, preferred_element_type=F32)
        key_raw = jnp.dot(normed1, w_key, preferred_element_type=F32)
        value_rot = jnp.dot(normed1, w_value, preferred_element_type=F32).astype(BF)
        query_rot = head_prep(query_raw, q_gain, cosine_table, sine_table).astype(BF)
        key_rot = head_prep(key_raw, k_gain, cosine_table, sine_table).astype(BF)
        attn_mixed, lse = attend(query_rot, key_rot, value_rot, segments, kv_here, head_dim)
        partial_attn = jnp.dot(attn_mixed, w_out, preferred_element_type=F32)
        x_own = own(layer_input).astype(F32)
        residual = x_own + reduce_tensor(split_relative(partial_attn), F32, F32)
        normed2 = rms_scale(residual, ffn_gain).astype(BF)

        normed_all = gather_tokens(normed2)
        attn_all = gather_batches(jnp.concatenate(split_relative(attn_mixed), axis=0))

        def dense_weights(rows, chosen):
            logits = jnp.dot(rows, router, preferred_element_type=F32)
            marks = jnp.any(
                chosen[:, :, None] == jnp.arange(experts, dtype=jnp.int32)[None, None, :], axis=1
            )
            shown = jnp.where(marks, logits, -jnp.inf)
            power = jnp.exp(shown - jnp.max(shown, axis=-1, keepdims=True))
            return power / jnp.sum(power, axis=-1, keepdims=True)

        weights_all = dense_weights(normed_all, routes_all)
        weights_here = lax.dynamic_slice_in_dim(weights_all.T, first_expert, experts_here, axis=0)
        names = first_expert + jnp.arange(experts_here, dtype=jnp.int32)
        marks = jnp.any(routes_all.T[None] == names[:, None, None], axis=1)
        index = jnp.arange(row_count, dtype=jnp.int32)
        earlier = (index[:, None] < index[None, :]).astype(BF)
        grouped = marks.astype(BF).reshape(experts_here, n_dp, row_count)
        place = jnp.einsum("ebt,tu->ebu", grouped, earlier, preferred_element_type=F32)
        counts = jnp.sum(grouped.astype(F32), axis=2)
        batch_at = jnp.arange(n_dp)
        begins = jnp.sum(
            jnp.where(batch_at[:, None] > batch_at[None, :], counts[:, None, :], 0.0), axis=2
        )
        place = (place + begins[:, :, None]).astype(jnp.int32).reshape(experts_here, tokens)
        place = jnp.where(marks, place, -1)
        picks = place[:, None, :] == jnp.arange(slots, dtype=jnp.int32)[None, :, None]
        one_hot = picks.astype(BF).reshape(experts_here * slots, tokens)

        def to_slots(rows):
            packed = jnp.dot(one_hot, rows, preferred_element_type=F32).astype(BF)
            return packed.reshape(experts_here, slots, width)

        def to_tokens(packed):
            packed = packed.reshape(experts_here * slots, width)
            return lax.dot_general(
                one_hot, packed, (((0,), (0,)), ((), ())), preferred_element_type=F32
            ).astype(BF)

        slot_weight = jnp.sum(jnp.where(picks, weights_here[:, None, :], 0.0), axis=2)

        cot_in = to_slots(cot_all)
        raw_act = jnp.einsum("erd,efd->erf", cot_in, w_down, preferred_element_type=F32)
        expert_in = to_slots(normed_all)
        gate_pre = jnp.einsum("erd,edf->erf", expert_in, w_gate, preferred_element_type=F32)
        up_pre = jnp.einsum("erd,edf->erf", expert_in, w_up, preferred_element_type=F32)
        sigmoid_g = jax.nn.sigmoid(gate_pre)
        silu_g = gate_pre * sigmoid_g
        activation = (silu_g * up_pre).astype(BF).astype(F32)
        slot_dw = jnp.sum(activation * raw_act, axis=2)
        weighted = (activation * slot_weight[:, :, None]).astype(BF)
        d_act = raw_act * slot_weight[:, :, None]
        d_gate = (d_act * up_pre * sigmoid_g * (1.0 + gate_pre * (1.0 - sigmoid_g))).astype(BF)
        d_up = (d_act * silu_g).astype(BF)
        d_in = jnp.einsum("erf,edf->erd", d_gate, w_gate, preferred_element_type=F32)
        d_in = (
            d_in + jnp.einsum("erf,edf->erd", d_up, w_up, preferred_element_type=F32)
        ).astype(BF)
        d_weights = jnp.sum(jnp.where(picks, slot_dw[:, :, None], 0.0), axis=1)
        d_weights = lax.dynamic_update_slice(
            jnp.zeros((-(-experts // 128) * 128, tokens), F32), d_weights, (first_expert, 0)
        )
        back = jnp.concatenate([to_tokens(d_in), d_weights.T.astype(BF)], axis=1)
        back = reduce_tokens(back, own_rows)

        expert_out = jnp.einsum(
            "erf,efd->erd", weighted, w_down, preferred_element_type=F32
        ).astype(BF)
        moe = reduce_tokens(to_tokens(expert_out), own_rows)
        layer_out = (residual + moe).astype(BF)
        layer_out = jnp.concatenate(relative(over_tensor(layer_out)), axis=0)
        grad_down = jnp.einsum("erf,erd->efd", weighted, cot_in, preferred_element_type=F32)
        grad_gate = jnp.einsum("erd,erf->edf", expert_in, d_gate, preferred_element_type=F32)
        grad_up = jnp.einsum("erd,erf->edf", expert_in, d_up, preferred_element_type=F32)

        weights_own = dense_weights(normed2, own(routes))
        dw_own = back[:, width : width + experts]
        d_logits = weights_own * (dw_own - jnp.sum(weights_own * dw_own, axis=1, keepdims=True))
        d_logits = d_logits.astype(BF)
        d_norm2 = back[:, :width] + jnp.dot(d_logits, router.T, preferred_element_type=F32)
        d_resid_norm, grad_ffn_gain = jax.vjp(rms_scale, residual, ffn_gain)[1](d_norm2)
        d_resid = own(cotangent).astype(F32) + d_resid_norm
        pad = back.shape[1] - width - experts
        sent = jnp.concatenate(
            [d_resid.astype(BF), d_logits, jnp.zeros((own_rows, pad), BF)], axis=1
        )
        sent_all = gather_tokens(sent)
        d_resid_all = sent_all[:, :width]
        grad_router = lax.dot_general(
            normed_all,
            sent_all[:, width : width + experts],
            (((0,), (0,)), ((), ())),
            preferred_element_type=F32,
        )
        d_resid_bf = jnp.concatenate(split_relative(d_resid_all[:row_count]), axis=0)
        grad_out = lax.dot_general(
            attn_all, d_resid_all, (((0,), (0,)), ((), ())), preferred_element_type=F32
        )

        d_attn = jnp.dot(d_resid_bf, w_out.T, preferred_element_type=F32).astype(BF)
        d_qrot, d_krot, d_vals = attend_back(
            query_rot, key_rot, value_rot, segments, lse, d_attn, kv_here, head_dim
        )
        prep = lambda raw_in, gain_in: head_prep(raw_in, gain_in, cosine_table, sine_table)
        d_qraw, grad_qgain = jax.vjp(prep, query_raw, q_gain)[1](d_qrot)
        d_kraw, grad_kgain = jax.vjp(prep, key_raw, k_gain)[1](d_krot)
        d_qkv = jnp.concatenate([d_qraw.astype(BF), d_kraw.astype(BF), d_vals.astype(BF)], axis=1)
        d_qkv_all = gather_batches(jnp.concatenate(split_relative(d_qkv), axis=0))
        q_width = w_query.shape[1]
        k_width = w_key.shape[1]
        input_all, _ = lax.optimization_barrier((own(layer_input), normed_all))
        normed1_all = rms_scale(gather_tokens(input_all).astype(F32), attn_gain).astype(BF)

        def over_tokens(grads):
            return lax.dot_general(
                normed1_all, grads, (((0,), (0,)), ((), ())), preferred_element_type=F32
            )

        grad_query = over_tokens(d_qkv_all[:, :q_width])
        grad_key = over_tokens(d_qkv_all[:, q_width : q_width + k_width])
        grad_value = over_tokens(d_qkv_all[:, q_width + k_width :])
        d_norm1 = jnp.dot(d_qkv[:, :q_width], w_query.T, preferred_element_type=F32)
        d_norm1 = d_norm1 + jnp.dot(
            d_qkv[:, q_width : q_width + k_width], w_key.T, preferred_element_type=F32
        )
        d_norm1 = d_norm1 + jnp.dot(
            d_qkv[:, q_width + k_width :], w_value.T, preferred_element_type=F32
        )
        grad_attn_gain = jax.vjp(lambda gain: rms_scale(x_float, gain), attn_gain)[1](d_norm1)[0]
        d_norm1_own = reduce_tensor(split_relative(d_norm1.astype(BF)), BF, F32)
        d_x_norm = jax.vjp(lambda rows: rms_scale(rows, attn_gain), x_own)[1](d_norm1_own)[0]
        d_input = (d_resid + d_x_norm).astype(BF)
        d_input = jnp.concatenate(relative(over_tensor(d_input)), axis=0).astype(F32)
        gains = jnp.concatenate([grad_attn_gain, grad_ffn_gain, grad_qgain, grad_kgain])
        gains = sum_all(gains.reshape(-1, 128)).reshape(-1)
        return (
            layer_out,
            d_input,
            gains[:width],
            grad_query,
            grad_key,
            grad_value,
            gains[2 * width : 2 * width + head_dim],
            gains[2 * width + head_dim :],
            grad_out,
            gains[width : 2 * width],
            grad_router,
            grad_gate,
            grad_up,
            grad_down,
        )

    return on_device


def solution(mesh):
    in_specs = (
        P("dp", None),
        P("dp", None),
        P("dp", None),
        P("dp", None),
        P(),
        P(None, "tensor"),
        P(None, "tensor"),
        P(None, "tensor"),
        P(),
        P(),
        P("tensor", None),
        P(),
        P(),
        P("dp", None, "tensor"),
        P("dp", None, "tensor"),
        P("dp", "tensor", None),
    )
    out_specs = (
        P("dp", None),
        P("dp", None),
        P(),
        P(None, "tensor"),
        P(None, "tensor"),
        P(None, "tensor"),
        P(),
        P(),
        P("tensor", None),
        P(),
        P(),
        P("dp", None, "tensor"),
        P("dp", None, "tensor"),
        P("dp", "tensor", None),
    )
    return jax.shard_map(
        make_device_fn(mesh), mesh=mesh, in_specs=in_specs, out_specs=out_specs, check_vma=False
    )
```

time: 1830 us -> 679 us (0.37)
  the two profiles are of different devices: /device:TPU:0 before, /device:TPU:13 now
where the time goes in v1:
time: 679 us; the launch traced here: 670 us
  starting transfers between devices  247 us (36%)
  matrix products  191 us (28%)
  waiting for transfers between devices  160 us (24%)
  other arithmetic  34.3 us (5%)
  local copies, waits for them, and re-layouts  33.4 us (5%)
    ppermute x159, starting transfers between devices, flip(): return lax.ppermute(x, 'tensor', [(i, i ^ mask) for i in range(n_tp)])  141 us
    ppermute x70, starting transfers between devices, rot(): return lax.ppermute(x, 'dp', [(i, (i + step) % n_dp) for i in range(n_dp)])  106 us
    ppermute x70, waiting for transfers between devices, rot(): return lax.ppermute(x, 'dp', [(i, (i + step) % n_dp) for i in range(n_dp)])  86.5 us
    ppermute x159, waiting for transfers between devices, flip(): return lax.ppermute(x, 'tensor', [(i, i ^ mask) for i in range(n_tp)])  73.8 us
    dot_general x2, matrix products, to_tokens(): lax.dot_general(one_hot, packed, (((0,), (0,)), ((), ())), preferred_elem...  32.1 us
    dot_general x2, matrix products, to_slots(): packed = jnp.dot(one_hot, rows, preferred_element_type=F32).astype(BF)  26.9 us
    dot_general x3, matrix products, over_tokens(): lax.dot_general(normed1_all, grads, (((0,), (0,)), ((), ())), preferred_e...  18.7 us
    unnamed x309, local copies, waits for them, and re-layouts  17.8 us
  transfers between devices with their start and end apart: 229, of which 70 were waited for; matrix products, arithmetic and copies ran while one was open for 20% of the time, Pallas kernels for 0%

profile of v1, /device:TPU:13, one launch (start us, length us, event | category | flops | bytes accessed | tf_op | source)
XLA Modules:
  0.0 669.8 jit_solution(9395392120137976770)
XLA Ops:
  9.9 3.1 fusion.129
  21.9 2.9 fusion.146
  38.0 3.2 collective-permute-start.86
  41.8 2.9 iota_compare_fusion.18
  54.5 4.3 collective-permute-done.80
  63.5 25.6 %collective-permute-done.196 = bf16[128,1024]{1,0:T(8,128)(2,1)S(1)} collective-permute-done((bf16[128,1024]{1,0:T(8,128)(2,1)S(1)}, bf16[128,1024]{1,0:T(8,128)(2,1)S(1)}, u32[]{:S(2)}, u32[]{:S(2)}) %collective-permute-start.196) | collective-permute-done | bytes 262176 | tf_op jit(solution)/shard_map/ppermute | solution.py:92
  89.1 5.6 collective-permute-done.197
  94.7 3.2 collective-permute-start.90
  102.8 4.2 collective-permute-start.83
  108.4 3.8 collective-permute-done.84
  122.4 2.7 collective-permute-done.92
  136.7 13.3 %convolution_convert_fusion = bf16[2560,2048]{1,0:T(8,128)(2,1)} fusion(pred[2560,1024]{1,0:T(32,128)(4,1)S(1)} %bitcast_compare_fusion, bf16[1024,2048]{1,0:T(8,128)(2,1)S(1)} %constant_dynamic-update-slice_fusion.40), kind=kOutput, calls=%fused_computation.1 | convolution fusion | flops 10742661120 | bytes 17301504 | tf_op jit(solution)/shard_map/dot_general | solution.py:229
  152.9 4.7 collective-permute-start.21
  161.6 3.8 collective-permute-start.29
  196.7 13.6 %convolution_convert_fusion.1 = bf16[2560,2048]{1,0:T(8,128)(2,1)} fusion(pred[2560,1024]{1,0:T(32,128)(4,1)S(1)} %bitcast_compare_fusion, bf16[1024,2048]{1,0:T(8,128)(2,1)S(1)} %constant_dynamic-update-slice_fusion.8), kind=kOutput, calls=%fused_computation.2 | convolution fusion | flops 10742661120 | bytes 17301504 | tf_op jit(solution)/shard_map/dot_general | solution.py:229
  211.8 11.4 %fusion.147 = f32[8,320,192]{1,2,0:T(8,128)} fusion(bf16[8,320,2048]{2,1,0:T(8,128)(2,1)} %bitcast.462, bf16[8,2048,192]{1,2,0:T(8,128)(2,1)} %param.29), kind=kOutput, calls=%fused_computation.578 | convolution fusion | flops 2013265920 | bytes 18743296 | tf_op jit(solution)/shard_map/erd,edf->erf/dot_general | solution.py:243
  223.2 11.4 %fusion.148 = f32[8,320,192]{1,2,0:T(8,128)} fusion(bf16[8,320,2048]{2,1,0:T(8,128)(2,1)} %bitcast.463, bf16[8,2048,192]{1,2,0:T(8,128)(2,1)} %param.30), kind=kOutput, calls=%fused_computation.579 | convolution fusion | flops 2013265920 | bytes 18743296 | tf_op jit(solution)/shard_map/erd,edf->erf/dot_general | solution.py:244
  234.6 12.8 %fusion.17 = (f32[8,320]{1,0:T(8,128)S(1)}, bf16[8,320,192]{1,2,0:T(8,128)(2,1)S(1)}, f32[8,320,192]{1,2,0:T(8,128)}) fusion(f32[8,320,192]{1,2,0:T(8,128)} %fusion.148, f32[8,320,192]{1,2,0:T(8,128)} %fusion.147, bf16[8,320,2048]{2,1,0:T(8,128)(2,1)} %bitcast.473, bf16[8,192,2048]{2,1,0:T(8,128)(2,1)} %param.31), kind=kOutput, calls=%fused_computation.29 | convolution fusion | flops 2017687040 | bytes 23668736 | tf_op jit(solution)/shard_map/erd,efd->erf/dot_general | solution.py:241
  247.4 2.9 select_reduce_fusion
  250.3 12.2 %fusion.35 = f32[8,192,2048]{2,1,0:T(8,128)} fusion(bf16[8,320,2048]{2,1,0:T(8,128)(2,1)} %bitcast.474, bf16[8,320,192]{1,2,0:T(8,128)(2,1)S(1)} %get-tuple-element.34, f32[8,320]{1,0:T(8,128)S(1)} %get-tuple-element.25), kind=kOutput, calls=%fused_computation.65 | convolution fusion | flops 2014740480 | bytes 24061952 | tf_op jit(solution)/shard_map/erf,erd->efd/dot_general | solution.py:270
  262.5 6.1 fusion.222
  268.6 5.8 multiply_convert_fusion
  274.4 13.2 %fusion.149 = f32[8,320,2048]{2,1,0:T(8,128)} fusion(bf16[8,320,192]{1,2,0:T(8,128)(2,1)} %get-tuple-element.45, bf16[8,2048,192]{1,2,0:T(8,128)(2,1)} %param.29), kind=kOutput, calls=%fused_computation.580 | convolution fusion | flops 2013265920 | bytes 28246016 | tf_op jit(solution)/shard_map/erf,edf->erd/dot_general | solution.py:253
  287.7 8.1 %fusion.151 = f32[8,2048,192]{1,2,0:T(8,128)} fusion(bf16[8,320,192]{1,2,0:T(8,128)(2,1)} %get-tuple-element.45, bf16[8,320,2048]{2,1,0:T(8,128)(2,1)S(1)} %bitcast.467), kind=kOutput, calls=%fused_computation.582 | convolution fusion | flops 2013265920 | bytes 24051712 | tf_op jit(solution)/shard_map/erd,erf->edf/dot_general | solution.py:271
  295.8 12.2 %bitcast_convert_fusion.1 = bf16[1024,2048]{1,0:T(8,128)(2,1)S(1)} fusion(s32[8,1024]{1,0:T(8,128)S(1)} %bitcast_select_fusion, bf16[8,320,2048]{2,1,0:T(8,128)(2,1)S(1)} %fusion.222), kind=kOutput, calls=%fused_computation.16 | convolution fusion | flops 10742136832 | bytes 14712832 | tf_op jit(solution)/shard_map/dot_general | solution.py:234
  312.6 12.2 %fusion.152 = f32[8,2048,192]{1,2,0:T(8,128)} fusion(bf16[8,320,192]{1,2,0:T(8,128)(2,1)S(1)} %copy-done.11, bf16[8,320,2048]{2,1,0:T(8,128)(2,1)} %bitcast.464), kind=kOutput, calls=%fused_computation.583 | convolution fusion | flops 2013265920 | bytes 24051712 | tf_op jit(solution)/shard_map/erd,erf->edf/dot_general | solution.py:272
  324.8 19.9 %bitcast_convert_fusion = bf16[1024,2048]{1,0:T(8,128)(2,1)} fusion(f32[8,320,2048]{2,1,0:T(8,128)} %fusion.149, bf16[8,320,192]{1,2,0:T(8,128)(2,1)S(1)} %copy-done.11, bf16[8,2048,192]{1,2,0:T(8,128)(2,1)} %param.30, pred[8,320,1024]{2,1,0:T(32,128)(4,1)} %iota_compare_fusion.18), kind=kOutput, calls=%fused_computation.15 | convolution fusion | flops 12763267072 | bytes 35061760 | tf_op jit(solution)/shard_map/dot_general | solution.py:234
  429.6 3.0 collective-permute-done.173
  461.1 10.3 %collective-permute-start.69 = (bf16[32,2048]{1,0:T(8,128)(2,1)S(1)}, bf16[32,2048]{1,0:T(8,128)(2,1)S(1)}, u32[]{:S(2)}, u32[]{:S(2)}) collective-permute-start(bf16[32,2048]{1,0:T(8,128)(2,1)S(1)} %get-tuple-element.76), channel_id=1, source_target_pairs={{0,1},{1,0},{2,3},{3,2},{4,5},{5,4},{6,7},{7,6},{8,9},{9,8},{10,11... | collective-permute-start | bytes 393224 | tf_op jit(solution)/shard_map/ppermute | solution.py:95
  471.9 4.1 collective-permute-start.48
  485.0 5.4 collective-permute-done.56
  490.4 3.0 collective-permute-done.60
  493.4 2.8 collective-permute-done.64
  499.0 2.7 collective-permute-start.139
  506.6 3.0 collective-permute-done.72
  513.4 3.7 convolution_convert_fusion.3
  537.8 4.2 collective-permute-start.209
  543.7 2.9 collective-permute-done.203
  546.6 3.7 collective-permute-start.153
  562.3 3.5 collective-permute-start.225
  588.1 6.9 %fusion.10 = f32[1024,2048]{1,0:T(8,128)} fusion(bf16[1024,1024]{1,0:T(8,128)(2,1)S(1)} %copy-done.71, bf16[1024,2176]{1,0:T(8,128)(2,1)S(1)} %constant_dynamic-update-slice_fusion.119), kind=kOutput, calls=%fused_computation.21 | convolution fusion | flops 4294967296 | bytes 14680064 | tf_op jit(solution)/shard_map/dot_general | solution.py:294
  601.4 27.4 %collective-permute-done.189 = bf16[128,1280]{0,1:T(8,128)(2,1)S(1)} collective-permute-done((bf16[128,1280]{0,1:T(8,128)(2,1)S(1)}, bf16[128,1280]{0,1:T(8,128)(2,1)S(1)}, u32[]{:S(2)}, u32[]{:S(2)}) %collective-permute-start.189) | collective-permute-done | bytes 327712 | tf_op jit(solution)/shard_map/ppermute | solution.py:92
  629.5 6.3 collective-permute-done.190
  639.4 3.1 collective-permute-done.193
  642.5 6.4 concatenate.108
  648.9 11.3 %fusion.19 = f32[2048,1024]{1,0:T(8,128)} fusion(bf16[1024,1280]{0,1:T(8,128)(2,1)} %concatenate.108, bf16[1024,2048]{1,0:T(8,128)(2,1)} %copy-done.12, f32[2048]{0:T(1024)S(1)} %copy-done.50, f32[1024]{0:T(1024)S(1)} %add_rsqrt_fusion), kind=kOutput, calls=%fused_computation.35 | convolution fusion | flops 4303355904 | bytes 14692352 | tf_op jit(solution)/shard_map/dot_general | solution.py:313
  660.1 3.7 fusion.78
  664.5 3.7 fusion.80
  (874 shorter events, 319.8 us)
Async XLA Ops:
  2.6 27.7 %collective-permute-start.3 = (s32[1,8,128]{2,1,0:T(8,128)S(1)}, s32[1,8,128]{2,1,0:T(8,128)S(1)}, u32[]{:S(2)}, u32[]{:S(2)}) collective-permute-start(s32[1,8,128]{2,1,0:T(8,128)S(1)} %get-tuple-element.43), channel_id=1, source_target_pairs={{0,4},{4,8},{8,12},{12,16},{16,20},{20,24},{24,28},{28,0},{1,5},{5... | collective-permute-start | bytes 12296 | tf_op jit(solution)/shard_map/ppermute | solution.py:92
  3.8 27.7 %collective-permute-start.4 = (s32[1,8,128]{2,1,0:T(8,128)S(1)}, s32[1,8,128]{2,1,0:T(8,128)S(1)}, u32[]{:S(2)}, u32[]{:S(2)}) collective-permute-start(s32[1,8,128]{2,1,0:T(8,128)S(1)} %get-tuple-element.43), channel_id=1, source_target_pairs={{0,8},{4,12},{8,16},{12,20},{16,24},{20,28},{24,0},{28,4},{1,9},{5... | collective-permute-start | bytes 12296 | tf_op jit(solution)/shard_map/ppermute | solution.py:92
  5.1 27.9 %collective-permute-start.5 = (s32[1,8,128]{2,1,0:T(8,128)S(1)}, s32[1,8,128]{2,1,0:T(8,128)S(1)}, u32[]{:S(2)}, u32[]{:S(2)}) collective-permute-start(s32[1,8,128]{2,1,0:T(8,128)S(1)} %get-tuple-element.43), channel_id=1, source_target_pairs={{0,12},{4,16},{8,20},{12,24},{16,28},{20,0},{24,4},{28,8},{1,13},{... | collective-permute-start | bytes 12296 | tf_op jit(solution)/shard_map/ppermute | solution.py:92
  6.1 29.5 %collective-permute-start.6 = (s32[1,8,128]{2,1,0:T(8,128)S(1)}, s32[1,8,128]{2,1,0:T(8,128)S(1)}, u32[]{:S(2)}, u32[]{:S(2)}) collective-permute-start(s32[1,8,128]{2,1,0:T(8,128)S(1)} %get-tuple-element.43), channel_id=1, source_target_pairs={{0,16},{4,20},{8,24},{12,28},{16,0},{20,4},{24,8},{28,12},{1,17},{... | collective-permute-start | bytes 12296 | tf_op jit(solution)/shard_map/ppermute | solution.py:92
  7.5 29.4 %collective-permute-start.7 = (s32[1,8,128]{2,1,0:T(8,128)S(1)}, s32[1,8,128]{2,1,0:T(8,128)S(1)}, u32[]{:S(2)}, u32[]{:S(2)}) collective-permute-start(s32[1,8,128]{2,1,0:T(8,128)S(1)} %get-tuple-element.43), channel_id=1, source_target_pairs={{0,20},{4,24},{8,28},{12,0},{16,4},{20,8},{24,12},{28,16},{1,21},{... | collective-permute-start | bytes 12296 | tf_op jit(solution)/shard_map/ppermute | solution.py:92
  37.6 63.0 %collective-permute-start.82 = (bf16[32,2048]{1,0:T(8,128)(2,1)S(1)}, bf16[32,2048]{1,0:T(8,128)(2,1)S(1)}, u32[]{:S(2)}, u32[]{:S(2)}) collective-permute-start(bf16[32,2048]{1,0:T(8,128)(2,1)S(1)} %get-tuple-element.36), channel_id=1, source_target_pairs={{0,8},{4,12},{8,16},{12,20},{16,24},{20,28},{24,0},{28,4},{1,9},{5... | collective-permute-start | bytes 393224 | tf_op jit(solution)/shard_map/ppermute | solution.py:92
  38.0 69.7 %collective-permute-start.86 = (bf16[32,2048]{1,0:T(8,128)(2,1)S(1)}, bf16[32,2048]{1,0:T(8,128)(2,1)S(1)}, u32[]{:S(2)}, u32[]{:S(2)}) collective-permute-start(bf16[32,2048]{1,0:T(8,128)(2,1)S(1)} %get-tuple-element.36), channel_id=1, source_target_pairs={{0,12},{4,16},{8,20},{12,24},{16,28},{20,0},{24,4},{28,8},{1,13},{... | collective-permute-start | bytes 393224 | tf_op jit(solution)/shard_map/ppermute | solution.py:92
  58.8 30.3 %collective-permute-start.196 = (bf16[128,1024]{1,0:T(8,128)(2,1)S(1)}, bf16[128,1024]{1,0:T(8,128)(2,1)S(1)}, u32[]{:S(2)}, u32[]{:S(2)}) collective-permute-start(bf16[128,1024]{1,0:T(8,128)(2,1)S(1)} %copy-done.56), channel_id=1, source_target_pairs={{0,12},{4,16},{8,20},{12,24},{16,28},{20,0},{24,4},{28,8},{1,13},{... | collective-permute-start | bytes 786440 | tf_op jit(solution)/shard_map/ppermute | solution.py:92
  59.5 35.2 %collective-permute-start.197 = (bf16[128,1024]{1,0:T(8,128)(2,1)S(1)}, bf16[128,1024]{1,0:T(8,128)(2,1)S(1)}, u32[]{:S(2)}, u32[]{:S(2)}) collective-permute-start(bf16[128,1024]{1,0:T(8,128)(2,1)S(1)} %copy-done.56), channel_id=1, source_target_pairs={{0,16},{4,20},{8,24},{12,28},{16,0},{20,4},{24,8},{28,12},{1,17},{... | collective-permute-start | bytes 786440 | tf_op jit(solution)/shard_map/ppermute | solution.py:92
  62.8 31.9 %collective-permute-start.198 = (bf16[128,1024]{1,0:T(8,128)(2,1)S(1)}, bf16[128,1024]{1,0:T(8,128)(2,1)S(1)}, u32[]{:S(2)}, u32[]{:S(2)}) collective-permute-start(bf16[128,1024]{1,0:T(8,128)(2,1)S(1)} %copy-done.56), channel_id=1, source_target_pairs={{0,20},{4,24},{8,28},{12,0},{16,4},{20,8},{24,12},{28,16},{1,21},{... | collective-permute-start | bytes 786440 | tf_op jit(solution)/shard_map/ppermute | solution.py:92
  94.7 19.9 %collective-permute-start.90 = (bf16[32,2048]{1,0:T(8,128)(2,1)S(1)}, bf16[32,2048]{1,0:T(8,128)(2,1)S(1)}, u32[]{:S(2)}, u32[]{:S(2)}) collective-permute-start(bf16[32,2048]{1,0:T(8,128)(2,1)S(1)} %get-tuple-element.36), channel_id=1, source_target_pairs={{0,16},{4,20},{8,24},{12,28},{16,0},{20,4},{24,8},{28,12},{1,17},{... | collective-permute-start | bytes 393224 | tf_op jit(solution)/shard_map/ppermute | solution.py:92
  100.6 19.3 %collective-permute-start.94 = (bf16[32,2048]{1,0:T(8,128)(2,1)S(1)}, bf16[32,2048]{1,0:T(8,128)(2,1)S(1)}, u32[]{:S(2)}, u32[]{:S(2)}) collective-permute-start(bf16[32,2048]{1,0:T(8,128)(2,1)S(1)} %get-tuple-element.36), channel_id=1, source_target_pairs={{0,20},{4,24},{8,28},{12,0},{16,4},{20,8},{24,12},{28,16},{1,21},{... | collective-permute-start | bytes 393224 | tf_op jit(solution)/shard_map/ppermute | solution.py:92
  129.9 20.1 %collective-permute-start = (f32[32,2048]{1,0:T(8,128)S(1)}, f32[32,2048]{1,0:T(8,128)S(1)}, u32[]{:S(2)}, u32[]{:S(2)}) collective-permute-start(f32[32,2048]{1,0:T(8,128)S(1)} %get-tuple-element.108), channel_id=1, source_target_pairs={{0,1},{1,0},{2,3},{3,2},{4,5},{5,4},{6,7},{7,6},{8,9},{9,8},{10,11... | collective-permute-start | bytes 786440 | tf_op jit(solution)/shard_map/ppermute | solution.py:95
  130.3 19.7 %collective-permute-start.2 = (f32[32,2048]{1,0:T(8,128)S(1)}, f32[32,2048]{1,0:T(8,128)S(1)}, u32[]{:S(2)}, u32[]{:S(2)}) collective-permute-start(f32[32,2048]{1,0:T(8,128)S(1)} %get-tuple-element.109), channel_id=1, source_target_pairs={{0,2},{1,3},{2,0},{3,1},{4,6},{5,7},{6,4},{7,5},{8,10},{9,11},{10,... | collective-permute-start | bytes 786440 | tf_op jit(solution)/shard_map/ppermute | solution.py:95
  152.9 15.6 %collective-permute-start.21 = (bf16[32,2048]{1,0:T(8,128)(2,1)S(1)}, bf16[32,2048]{1,0:T(8,128)(2,1)S(1)}, u32[]{:S(2)}, u32[]{:S(2)}) collective-permute-start(bf16[32,2048]{1,0:T(8,128)(2,1)S(1)} %get-tuple-element.38), channel_id=1, source_target_pairs={{0,12},{4,16},{8,20},{12,24},{16,28},{20,0},{24,4},{28,8},{1,13},{... | collective-permute-start | bytes 393224 | tf_op jit(solution)/shard_map/ppermute | solution.py:92
  158.6 16.7 %collective-permute-start.25 = (bf16[32,2048]{1,0:T(8,128)(2,1)S(1)}, bf16[32,2048]{1,0:T(8,128)(2,1)S(1)}, u32[]{:S(2)}, u32[]{:S(2)}) collective-permute-start(bf16[32,2048]{1,0:T(8,128)(2,1)S(1)} %get-tuple-element.38), channel_id=1, source_target_pairs={{0,16},{4,20},{8,24},{12,28},{16,0},{20,4},{24,8},{28,12},{1,17},{... | collective-permute-start | bytes 393224 | tf_op jit(solution)/shard_map/ppermute | solution.py:92
  161.6 18.9 %collective-permute-start.29 = (bf16[32,2048]{1,0:T(8,128)(2,1)S(1)}, bf16[32,2048]{1,0:T(8,128)(2,1)S(1)}, u32[]{:S(2)}, u32[]{:S(2)}) collective-permute-start(bf16[32,2048]{1,0:T(8,128)(2,1)S(1)} %get-tuple-element.38), channel_id=1, source_target_pairs={{0,20},{4,24},{8,28},{12,0},{16,4},{20,8},{24,12},{28,16},{1,21},{... | collective-permute-start | bytes 393224 | tf_op jit(solution)/shard_map/ppermute | solution.py:92
  311.0 38.4 %collective-permute-start.42 = (bf16[32,2048]{1,0:T(8,128)(2,1)}, bf16[32,2048]{1,0:T(8,128)(2,1)S(1)}, u32[]{:S(2)}, u32[]{:S(2)}) collective-permute-start(bf16[32,2048]{1,0:T(8,128)(2,1)} %get-tuple-element.90), channel_id=1, source_target_pairs={{0,1},{1,0},{2,3},{3,2},{4,5},{5,4},{6,7},{7,6},{8,9},{9,8},{10,11... | collective-permute-start | bytes 393224 | tf_op jit(solution)/shard_map/ppermute | solution.py:95
  311.4 38.3 %collective-permute-start.46 = (bf16[32,2048]{1,0:T(8,128)(2,1)}, bf16[32,2048]{1,0:T(8,128)(2,1)S(1)}, u32[]{:S(2)}, u32[]{:S(2)}) collective-permute-start(bf16[32,2048]{1,0:T(8,128)(2,1)} %get-tuple-element.88), channel_id=1, source_target_pairs={{0,1},{1,0},{2,3},{3,2},{4,5},{5,4},{6,7},{7,6},{8,9},{9,8},{10,11... | collective-permute-start | bytes 393224 | tf_op jit(solution)/shard_map/ppermute | solution.py:95
  311.6 38.7 %collective-permute-start.50 = (bf16[32,2048]{1,0:T(8,128)(2,1)}, bf16[32,2048]{1,0:T(8,128)(2,1)}, u32[]{:S(2)}, u32[]{:S(2)}) collective-permute-start(bf16[32,2048]{1,0:T(8,128)(2,1)} %get-tuple-element.86), channel_id=1, source_target_pairs={{0,1},{1,0},{2,3},{3,2},{4,5},{5,4},{6,7},{7,6},{8,9},{9,8},{10,11... | collective-permute-start | bytes 393224 | tf_op jit(solution)/shard_map/ppermute | solution.py:95
  311.9 38.7 %collective-permute-start.54 = (bf16[32,2048]{1,0:T(8,128)(2,1)}, bf16[32,2048]{1,0:T(8,128)(2,1)}, u32[]{:S(2)}, u32[]{:S(2)}) collective-permute-start(bf16[32,2048]{1,0:T(8,128)(2,1)} %get-tuple-element.84), channel_id=1, source_target_pairs={{0,1},{1,0},{2,3},{3,2},{4,5},{5,4},{6,7},{7,6},{8,9},{9,8},{10,11... | collective-permute-start | bytes 393224 | tf_op jit(solution)/shard_map/ppermute | solution.py:95
  312.1 38.8 %collective-permute-start.58 = (bf16[32,2048]{1,0:T(8,128)(2,1)}, bf16[32,2048]{1,0:T(8,128)(2,1)}, u32[]{:S(2)}, u32[]{:S(2)}) collective-permute-start(bf16[32,2048]{1,0:T(8,128)(2,1)} %get-tuple-element.82), channel_id=1, source_target_pairs={{0,1},{1,0},{2,3},{3,2},{4,5},{5,4},{6,7},{7,6},{8,9},{9,8},{10,11... | collective-permute-start | bytes 393224 | tf_op jit(solution)/shard_map/ppermute | solution.py:95
  389.2 14.9 %collective-permute-start.128 = (bf16[32,2176]{1,0:T(8,128)(2,1)S(1)}, bf16[32,2176]{1,0:T(8,128)(2,1)S(1)}, u32[]{:S(2)}, u32[]{:S(2)}) collective-permute-start(bf16[32,2176]{1,0:T(8,128)(2,1)S(1)} %get-tuple-element.64), channel_id=1, source_target_pairs={{0,2},{1,3},{2,0},{3,1},{4,6},{5,7},{6,4},{7,5},{8,10},{9,11},{10,... | collective-permute-start | bytes 417800 | tf_op jit(solution)/shard_map/ppermute | solution.py:95
  392.1 14.9 %collective-permute-start.132 = (bf16[32,2176]{1,0:T(8,128)(2,1)S(1)}, bf16[32,2176]{1,0:T(8,128)(2,1)S(1)}, u32[]{:S(2)}, u32[]{:S(2)}) collective-permute-start(bf16[32,2176]{1,0:T(8,128)(2,1)S(1)} %get-tuple-element.63), channel_id=1, source_target_pairs={{0,2},{1,3},{2,0},{3,1},{4,6},{5,7},{6,4},{7,5},{8,10},{9,11},{10,... | collective-permute-start | bytes 417800 | tf_op jit(solution)/shard_map/ppermute | solution.py:95
  398.1 16.9 %collective-permute-start.167 = (bf16[32,2048]{1,0:T(8,128)(2,1)S(1)}, bf16[32,2048]{1,0:T(8,128)(2,1)S(1)}, u32[]{:S(2)}, u32[]{:S(2)}) collective-permute-start(bf16[32,2048]{1,0:T(8,128)(2,1)S(1)} %get-tuple-element.15), channel_id=1, source_target_pairs={{0,12},{4,16},{8,20},{12,24},{16,28},{20,0},{24,4},{28,8},{1,13},{... | collective-permute-start | bytes 393224 | tf_op jit(solution)/shard_map/ppermute | solution.py:92
  401.1 20.8 %collective-permute-start.171 = (bf16[32,2048]{1,0:T(8,128)(2,1)S(1)}, bf16[32,2048]{1,0:T(8,128)(2,1)S(1)}, u32[]{:S(2)}, u32[]{:S(2)}) collective-permute-start(bf16[32,2048]{1,0:T(8,128)(2,1)S(1)} %get-tuple-element.15), channel_id=1, source_target_pairs={{0,16},{4,20},{8,24},{12,28},{16,0},{20,4},{24,8},{28,12},{1,17},{... | collective-permute-start | bytes 393224 | tf_op jit(solution)/shard_map/ppermute | solution.py:92
  408.3 20.5 %collective-permute-start.175 = (bf16[32,2048]{1,0:T(8,128)(2,1)S(1)}, bf16[32,2048]{1,0:T(8,128)(2,1)S(1)}, u32[]{:S(2)}, u32[]{:S(2)}) collective-permute-start(bf16[32,2048]{1,0:T(8,128)(2,1)S(1)} %get-tuple-element.15), channel_id=1, source_target_pairs={{0,20},{4,24},{8,28},{12,0},{16,4},{20,8},{24,12},{28,16},{1,21},{... | collective-permute-start | bytes 393224 | tf_op jit(solution)/shard_map/ppermute | solution.py:92
  415.0 18.9 %collective-permute-start.179 = (bf16[32,2048]{1,0:T(8,128)(2,1)S(1)}, bf16[32,2048]{1,0:T(8,128)(2,1)S(1)}, u32[]{:S(2)}, u32[]{:S(2)}) collective-permute-start(bf16[32,2048]{1,0:T(8,128)(2,1)S(1)} %get-tuple-element.15), channel_id=1, source_target_pairs={{0,24},{4,28},{8,0},{12,4},{16,8},{20,12},{24,16},{28,20},{1,25},{... | collective-permute-start | bytes 393224 | tf_op jit(solution)/shard_map/ppermute | solution.py:92
  428.8 25.8 %collective-permute-start.134 = (bf16[32,2176]{1,0:T(8,128)(2,1)S(1)}, bf16[32,2176]{1,0:T(8,128)(2,1)S(1)}, u32[]{:S(2)}, u32[]{:S(2)}) collective-permute-start(bf16[32,2176]{1,0:T(8,128)(2,1)S(1)} %get-tuple-element.46), channel_id=1, source_target_pairs={{0,1},{1,0},{2,3},{3,2},{4,5},{5,4},{6,7},{7,6},{8,9},{9,8},{10,11... | collective-permute-start | bytes 417800 | tf_op jit(solution)/shard_map/ppermute | solution.py:95
  454.6 16.7 %collective-permute-start.121 = (bf16[32,2176]{1,0:T(8,128)(2,1)S(1)}, bf16[32,2176]{1,0:T(8,128)(2,1)S(1)}, u32[]{:S(2)}, u32[]{:S(2)}) collective-permute-start(bf16[32,2176]{1,0:T(8,128)(2,1)S(1)} %get-tuple-element.74), channel_id=1, source_target_pairs={{0,16},{4,20},{8,24},{12,28},{16,0},{20,4},{24,8},{28,12},{1,17},{... | collective-permute-start | bytes 417800 | tf_op jit(solution)/shard_map/ppermute | solution.py:92
  454.7 17.3 %collective-permute-start.125 = (bf16[32,2176]{1,0:T(8,128)(2,1)S(1)}, bf16[32,2176]{1,0:T(8,128)(2,1)S(1)}, u32[]{:S(2)}, u32[]{:S(2)}) collective-permute-start(bf16[32,2176]{1,0:T(8,128)(2,1)S(1)} %get-tuple-element.73), channel_id=1, source_target_pairs={{0,12},{4,16},{8,20},{12,24},{16,28},{20,0},{24,4},{28,8},{1,13},{... | collective-permute-start | bytes 417800 | tf_op jit(solution)/shard_map/ppermute | solution.py:92
  456.4 19.6 %collective-permute-start.129 = (bf16[32,2176]{1,0:T(8,128)(2,1)S(1)}, bf16[32,2176]{1,0:T(8,128)(2,1)S(1)}, u32[]{:S(2)}, u32[]{:S(2)}) collective-permute-start(bf16[32,2176]{1,0:T(8,128)(2,1)S(1)} %get-tuple-element.72), channel_id=1, source_target_pairs={{0,8},{4,12},{8,16},{12,20},{16,24},{20,28},{24,0},{28,4},{1,9},{5... | collective-permute-start | bytes 417800 | tf_op jit(solution)/shard_map/ppermute | solution.py:92
  458.0 20.0 %collective-permute-start.133 = (bf16[32,2176]{1,0:T(8,128)(2,1)S(1)}, bf16[32,2176]{1,0:T(8,128)(2,1)S(1)}, u32[]{:S(2)}, u32[]{:S(2)}) collective-permute-start(bf16[32,2176]{1,0:T(8,128)(2,1)S(1)} %get-tuple-element.71), channel_id=1, source_target_pairs={{0,4},{4,8},{8,12},{12,16},{16,20},{20,24},{24,28},{28,0},{1,5},{5... | collective-permute-start | bytes 417800 | tf_op jit(solution)/shard_map/ppermute | solution.py:92
  461.1 18.2 %collective-permute-start.69 = (bf16[32,2048]{1,0:T(8,128)(2,1)S(1)}, bf16[32,2048]{1,0:T(8,128)(2,1)S(1)}, u32[]{:S(2)}, u32[]{:S(2)}) collective-permute-start(bf16[32,2048]{1,0:T(8,128)(2,1)S(1)} %get-tuple-element.76), channel_id=1, source_target_pairs={{0,1},{1,0},{2,3},{3,2},{4,5},{5,4},{6,7},{7,6},{8,9},{9,8},{10,11... | collective-permute-start | bytes 393224 | tf_op jit(solution)/shard_map/ppermute | solution.py:95
  483.4 15.1 %collective-permute-start.68 = (bf16[32,2048]{1,0:T(8,128)(2,1)S(1)}, bf16[32,2048]{1,0:T(8,128)(2,1)S(1)}, u32[]{:S(2)}, u32[]{:S(2)}) collective-permute-start(bf16[32,2048]{1,0:T(8,128)(2,1)S(1)} %get-tuple-element.101), channel_id=1, source_target_pairs={{0,4},{4,8},{8,12},{12,16},{16,20},{20,24},{24,28},{28,0},{1,5},{5... | collective-permute-start | bytes 393224 | tf_op jit(solution)/shard_map/ppermute | solution.py:92
  511.9 20.0 %collective-permute-start.202 = (bf16[32,2176]{1,0:T(8,128)(2,1)}, bf16[32,2176]{1,0:T(8,128)(2,1)}, u32[]{:S(2)}, u32[]{:S(2)}) collective-permute-start(bf16[32,2176]{1,0:T(8,128)(2,1)} %collective-permute-done.201), channel_id=1, source_target_pairs={{0,1},{1,0},{2,3},{3,2},{4,5},{5,4},{6,7},{7,6},{8,9},{9,8},{10,11... | collective-permute-start | bytes 417800 | tf_op jit(solution)/shard_map/ppermute | solution.py:95
  537.8 17.4 %collective-permute-start.209 = (bf16[32,2176]{1,0:T(8,128)(2,1)S(1)}, bf16[32,2176]{1,0:T(8,128)(2,1)S(1)}, u32[]{:S(2)}, u32[]{:S(2)}) collective-permute-start(bf16[32,2176]{1,0:T(8,128)(2,1)S(1)} %copy-done.26), channel_id=1, source_target_pairs={{0,12},{4,16},{8,20},{12,24},{16,28},{20,0},{24,4},{28,8},{1,13},{... | collective-permute-start | bytes 417800 | tf_op jit(solution)/shard_map/ppermute | solution.py:92
  542.0 20.2 %collective-permute-start.213 = (bf16[32,2176]{1,0:T(8,128)(2,1)S(1)}, bf16[32,2176]{1,0:T(8,128)(2,1)S(1)}, u32[]{:S(2)}, u32[]{:S(2)}) collective-permute-start(bf16[32,2176]{1,0:T(8,128)(2,1)S(1)} %copy-done.26), channel_id=1, source_target_pairs={{0,16},{4,20},{8,24},{12,28},{16,0},{20,4},{24,8},{28,12},{1,17},{... | collective-permute-start | bytes 417800 | tf_op jit(solution)/shard_map/ppermute | solution.py:92
  551.0 16.5 %collective-permute-start.217 = (bf16[32,2176]{1,0:T(8,128)(2,1)S(1)}, bf16[32,2176]{1,0:T(8,128)(2,1)S(1)}, u32[]{:S(2)}, u32[]{:S(2)}) collective-permute-start(bf16[32,2176]{1,0:T(8,128)(2,1)S(1)} %copy-done.26), channel_id=1, source_target_pairs={{0,20},{4,24},{8,28},{12,0},{16,4},{20,8},{24,12},{28,16},{1,21},{... | collective-permute-start | bytes 417800 | tf_op jit(solution)/shard_map/ppermute | solution.py:92
  577.9 22.8 %collective-permute-start.187 = (bf16[128,1280]{0,1:T(8,128)(2,1)S(1)}, bf16[128,1280]{0,1:T(8,128)(2,1)S(1)}, u32[]{:S(2)}, u32[]{:S(2)}) collective-permute-start(bf16[128,1280]{0,1:T(8,128)(2,1)S(1)} %pad_maximum_fusion.3), channel_id=1, source_target_pairs={{0,4},{4,8},{8,12},{12,16},{16,20},{20,24},{24,28},{28,0},{1,5},{5... | collective-permute-start | bytes 983048 | tf_op jit(solution)/shard_map/ppermute | solution.py:92
  580.0 20.8 %collective-permute-start.188 = (bf16[128,1280]{0,1:T(8,128)(2,1)S(1)}, bf16[128,1280]{0,1:T(8,128)(2,1)S(1)}, u32[]{:S(2)}, u32[]{:S(2)}) collective-permute-start(bf16[128,1280]{0,1:T(8,128)(2,1)S(1)} %pad_maximum_fusion.3), channel_id=1, source_target_pairs={{0,8},{4,12},{8,16},{12,20},{16,24},{20,28},{24,0},{28,4},{1,9},{5... | collective-permute-start | bytes 983048 | tf_op jit(solution)/shard_map/ppermute | solution.py:92
  583.5 45.3 %collective-permute-start.189 = (bf16[128,1280]{0,1:T(8,128)(2,1)S(1)}, bf16[128,1280]{0,1:T(8,128)(2,1)S(1)}, u32[]{:S(2)}, u32[]{:S(2)}) collective-permute-start(bf16[128,1280]{0,1:T(8,128)(2,1)S(1)} %pad_maximum_fusion.3), channel_id=1, source_target_pairs={{0,12},{4,16},{8,20},{12,24},{16,28},{20,0},{24,4},{28,8},{1,13},{... | collective-permute-start | bytes 983048 | tf_op jit(solution)/shard_map/ppermute | solution.py:92
  596.7 39.1 %collective-permute-start.190 = (bf16[128,1280]{0,1:T(8,128)(2,1)S(1)}, bf16[128,1280]{0,1:T(8,128)(2,1)S(1)}, u32[]{:S(2)}, u32[]{:S(2)}) collective-permute-start(bf16[128,1280]{0,1:T(8,128)(2,1)S(1)} %pad_maximum_fusion.3), channel_id=1, source_target_pairs={{0,16},{4,20},{8,24},{12,28},{16,0},{20,4},{24,8},{28,12},{1,17},{... | collective-permute-start | bytes 983048 | tf_op jit(solution)/shard_map/ppermute | solution.py:92
  598.9 38.8 %collective-permute-start.191 = (bf16[128,1280]{0,1:T(8,128)(2,1)S(1)}, bf16[128,1280]{0,1:T(8,128)(2,1)}, u32[]{:S(2)}, u32[]{:S(2)}) collective-permute-start(bf16[128,1280]{0,1:T(8,128)(2,1)S(1)} %pad_maximum_fusion.3), channel_id=1, source_target_pairs={{0,20},{4,24},{8,28},{12,0},{16,4},{20,8},{24,12},{28,16},{1,21},{... | collective-permute-start | bytes 983048 | tf_op jit(solution)/shard_map/ppermute | solution.py:92
  600.7 38.7 %collective-permute-start.192 = (bf16[128,1280]{0,1:T(8,128)(2,1)S(1)}, bf16[128,1280]{0,1:T(8,128)(2,1)}, u32[]{:S(2)}, u32[]{:S(2)}) collective-permute-start(bf16[128,1280]{0,1:T(8,128)(2,1)S(1)} %pad_maximum_fusion.3), channel_id=1, source_target_pairs={{0,24},{4,28},{8,0},{12,4},{16,8},{20,12},{24,16},{28,20},{1,25},{... | collective-permute-start | bytes 983048 | tf_op jit(solution)/shard_map/ppermute | solution.py:92
  600.9 41.6 %collective-permute-start.193 = (bf16[128,1280]{0,1:T(8,128)(2,1)S(1)}, bf16[128,1280]{0,1:T(8,128)(2,1)}, u32[]{:S(2)}, u32[]{:S(2)}) collective-permute-start(bf16[128,1280]{0,1:T(8,128)(2,1)S(1)} %pad_maximum_fusion.3), channel_id=1, source_target_pairs={{0,28},{4,0},{8,4},{12,8},{16,12},{20,16},{24,20},{28,24},{1,29},{... | collective-permute-start | bytes 983048 | tf_op jit(solution)/shard_map/ppermute | solution.py:92
  628.8 35.1 %collective-permute-start.143 = (bf16[32,2048]{1,0:T(8,128)(2,1)S(1)}, bf16[32,2048]{1,0:T(8,128)(2,1)S(1)}, u32[]{:S(2)}, u32[]{:S(2)}) collective-permute-start(bf16[32,2048]{1,0:T(8,128)(2,1)S(1)} %fusion.67), channel_id=1, source_target_pairs={{0,2},{1,3},{2,0},{3,1},{4,6},{5,7},{6,4},{7,5},{8,10},{9,11},{10,... | collective-permute-start | bytes 393224 | tf_op jit(solution)/shard_map/ppermute | solution.py:95
  636.5 31.7 %collective-permute-start.145 = (bf16[32,2048]{1,0:T(8,128)(2,1)S(1)}, bf16[32,2048]{1,0:T(8,128)(2,1)S(1)}, u32[]{:S(2)}, u32[]{:S(2)}) collective-permute-start(bf16[32,2048]{1,0:T(8,128)(2,1)S(1)} %fusion.67), channel_id=1, source_target_pairs={{0,1},{1,0},{2,3},{3,2},{4,5},{5,4},{6,7},{7,6},{8,9},{9,8},{10,11... | collective-permute-start | bytes 393224 | tf_op jit(solution)/shard_map/ppermute | solution.py:95
  (265 other events, 2319.5 us)

commit v2 on v1

--- a/solution.py
+++ b/solution.py
@@ -94,13 +94,18 @@
     def flip(x, mask):
         return lax.ppermute(x, "tensor", [(i, i ^ mask) for i in range(n_tp)])
 
+    groups = 2 if n_dp % 2 == 0 else 1
+    per = n_dp // groups
+    order = (0, 2, 1, 3)
+
+    def tied(x, marker):
+        return lax.optimization_barrier((x, marker))[0]
+
     def relative(quarters):
         own = lax.axis_index("tensor")
         for bit in (1, 2):
             on = (own & bit) != 0
-            quarters = [
-                jnp.where(on, quarters[q ^ bit], quarters[q]) for q in range(n_tp)
-            ]
+            quarters = [jnp.where(on, quarters[q ^ bit], quarters[q]) for q in range(n_tp)]
         return quarters
 
     def split_relative(x):
@@ -111,13 +116,32 @@
         return [x, flip(x, 1), across, flip(across, 1)]
 
     def gather_tokens(x):
-        blocks = []
-        for step in range(n_dp):
-            blocks.extend(over_tensor(x if step == 0 else rot(x, step)))
-        return jnp.concatenate(blocks, axis=0)
+        blocks = [x] + [rot(x, step) for step in range(1, n_dp)]
+        out = []
+        for g in range(groups):
+            held = over_tensor(jnp.concatenate(blocks[g * per : (g + 1) * per], axis=0))
+            out.extend(held[m] for m in order)
+        return jnp.concatenate(out, axis=0)
 
     def gather_batches(x):
-        return jnp.concatenate([x] + [rot(x, s) for s in range(1, n_dp)], axis=0)
+        rows = x[0].shape[0]
+        x = jnp.concatenate(x, axis=0)
+        blocks = [x] + [rot(x, step) for step in range(1, n_dp)]
+        return jnp.concatenate(
+            [
+                blocks[g * per + s][m * rows : (m + 1) * rows]
+                for g in range(groups)
+                for m in order
+                for s in range(per)
+            ],
+            axis=0,
+        )
+
+    def own_batch(x, rows):
+        parts = [None] * n_tp
+        for place, m in enumerate(order):
+            parts[m] = x[place * per * rows : place * per * rows + rows]
+        return jnp.concatenate(relative(parts), axis=0)
 
     def add_up(a, b, kind):
         return (a.astype(F32) + b.astype(F32)).astype(kind)
@@ -128,13 +152,20 @@
         return add_up(low, flip(high, 2), last)
 
     def reduce_tokens(x, rows):
-        grid = x.reshape(n_dp, n_tp, rows, x.shape[1])
+        grid = x.reshape(groups, 2, 2, per * rows, x.shape[1])
         total = None
-        for step in list(range(1, n_dp)) + [0]:
-            part = reduce_tensor([grid[step, m] for m in range(n_tp)], BF, BF)
-            part = part if step == 0 else rot(part, n_dp - step)
+        sums = [None] * n_dp
+        first = None
+        for g in reversed(range(groups)):
+            pair = add_up(grid[g, 0], flip(grid[g, 1], 1), BF)
+            first = pair if first is None else first
+            part = add_up(pair[0], flip(pair[1], 2), BF)
+            for s in range(per):
+                sums[g * per + s] = part[s * rows : (s + 1) * rows]
+        for step in list(range(n_dp - 1, 0, -1)) + [0]:
+            part = sums[step] if step == 0 else rot(sums[step], n_dp - step)
             total = part.astype(F32) if total is None else total + part.astype(F32)
-        return total
+        return total, first
 
     def sum_all(x):
         total = x
@@ -176,9 +207,11 @@
         def own(x):
             return lax.dynamic_slice_in_dim(x, first_row, own_rows, axis=0)
 
-        route_rows = jnp.concatenate(split_relative(routes), axis=0)
-        routes_all = gather_batches(route_rows.T.reshape(1, -1, row_count))
-        routes_all = jnp.transpose(routes_all, (0, 2, 1)).reshape(tokens, -1)
+        route_rows = jnp.concatenate(split_relative(routes), axis=0).T
+        route_rows = [route_rows] + [rot(route_rows, step) for step in range(1, n_dp)]
+        route_rows = jnp.stack(route_rows).reshape(groups, per, -1, n_tp, own_rows)
+        route_rows = route_rows[:, :, :, jnp.array(order)]
+        routes_all = jnp.transpose(route_rows, (0, 3, 1, 4, 2)).reshape(tokens, -1)
         cot_all = gather_tokens(own(cotangent))
 
         cosine_table, sine_table = rope_tables(seq_positions(segments), head_dim)
@@ -196,7 +229,8 @@
         normed2 = rms_scale(residual, ffn_gain).astype(BF)
 
         normed_all = gather_tokens(normed2)
-        attn_all = gather_batches(jnp.concatenate(split_relative(attn_mixed), axis=0))
+        later = tied((own(layer_input), tuple(split_relative(attn_mixed))), normed_all)
+        attn_all = gather_batches(list(later[1]))
 
         def dense_weights(rows, chosen):
             logits = jnp.dot(rows, router, preferred_element_type=F32)
@@ -239,6 +273,7 @@
 
         cot_in = to_slots(cot_all)
         raw_act = jnp.einsum("erd,efd->erf", cot_in, w_down, preferred_element_type=F32)
+        normed_all, raw_act = lax.optimization_barrier((normed_all, raw_act))
         expert_in = to_slots(normed_all)
         gate_pre = jnp.einsum("erd,edf->erf", expert_in, w_gate, preferred_element_type=F32)
         up_pre = jnp.einsum("erd,edf->erf", expert_in, w_up, preferred_element_type=F32)
@@ -259,15 +294,13 @@
             jnp.zeros((-(-experts // 128) * 128, tokens), F32), d_weights, (first_expert, 0)
         )
         back = jnp.concatenate([to_tokens(d_in), d_weights.T.astype(BF)], axis=1)
-        back = reduce_tokens(back, own_rows)
-
+        back, marker = reduce_tokens(back, own_rows)
+
+        expert_in, d_gate, d_up, weighted = tied((expert_in, d_gate, d_up, weighted), marker)
         expert_out = jnp.einsum(
             "erf,efd->erd", weighted, w_down, preferred_element_type=F32
         ).astype(BF)
-        moe = reduce_tokens(to_tokens(expert_out), own_rows)
-        layer_out = (residual + moe).astype(BF)
-        layer_out = jnp.concatenate(relative(over_tensor(layer_out)), axis=0)
-        grad_down = jnp.einsum("erf,erd->efd", weighted, cot_in, preferred_element_type=F32)
+        moe_terms = to_tokens(expert_out)
         grad_gate = jnp.einsum("erd,erf->edf", expert_in, d_gate, preferred_element_type=F32)
         grad_up = jnp.einsum("erd,erf->edf", expert_in, d_up, preferred_element_type=F32)
 
@@ -283,6 +316,11 @@
             [d_resid.astype(BF), d_logits, jnp.zeros((own_rows, pad), BF)], axis=1
         )
         sent_all = gather_tokens(sent)
+        weighted, cot_in = tied((weighted, cot_in), sent)
+        grad_down = jnp.einsum("erf,erd->efd", weighted, cot_in, preferred_element_type=F32)
+        moe = reduce_tokens(tied(moe_terms, sent_all), own_rows)[0]
+        layer_out = (residual + moe).astype(BF)
+        layer_out = jnp.concatenate(relative(over_tensor(layer_out)), axis=0)
         d_resid_all = sent_all[:, :width]
         grad_router = lax.dot_general(
             normed_all,
@@ -290,7 +328,7 @@
             (((0,), (0,)), ((), ())),
             preferred_element_type=F32,
         )
-        d_resid_bf = jnp.concatenate(split_relative(d_resid_all[:row_count]), axis=0)
+        d_resid_bf = own_batch(d_resid_all, own_rows)
         grad_out = lax.dot_general(
             attn_all, d_resid_all, (((0,), (0,)), ((), ())), preferred_element_type=F32
         )
@@ -303,11 +341,10 @@
         d_qraw, grad_qgain = jax.vjp(prep, query_raw, q_gain)[1](d_qrot)
         d_kraw, grad_kgain = jax.vjp(prep, key_raw, k_gain)[1](d_krot)
         d_qkv = jnp.concatenate([d_qraw.astype(BF), d_kraw.astype(BF), d_vals.astype(BF)], axis=1)
-        d_qkv_all = gather_batches(jnp.concatenate(split_relative(d_qkv), axis=0))
+        d_qkv_all = gather_batches(split_relative(d_qkv))
         q_width = w_query.shape[1]
         k_width = w_key.shape[1]
-        input_all, _ = lax.optimization_barrier((own(layer_input), normed_all))
-        normed1_all = rms_scale(gather_tokens(input_all).astype(F32), attn_gain).astype(BF)
+        normed1_all = rms_scale(gather_tokens(later[0]).astype(F32), attn_gain).astype(BF)
 
         def over_tokens(grads):
             return lax.dot_general(

time: 679 us -> 699 us (1.029)
  the two profiles are of different devices: /device:TPU:13 before, /device:TPU:0 now
where the time goes in v2:
time: 699 us; the launch traced here: 688 us
  waiting for transfers between devices  190 us (27%)
  matrix products  186 us (27%)
  starting transfers between devices  164 us (23%)
  local copies, waits for them, and re-layouts  98.6 us (14%)
  other arithmetic  46.9 us (7%)
    ppermute x70, starting transfers between devices, rot(): return lax.ppermute(x, 'dp', [(i, (i + step) % n_dp) for i in range(n_dp)])  143 us
    ppermute x70, waiting for transfers between devices, rot(): return lax.ppermute(x, 'dp', [(i, (i + step) % n_dp) for i in range(n_dp)])  106 us
    ppermute x47, waiting for transfers between devices, flip(): return lax.ppermute(x, 'tensor', [(i, i ^ mask) for i in range(n_tp)])  83.8 us
    unnamed x278, local copies, waits for them, and re-layouts  51.3 us
    dot_general x2, matrix products, to_tokens(): lax.dot_general(one_hot, packed, (((0,), (0,)), ((), ())), preferred_elem...  35.2 us
    dot_general x2, matrix products, to_slots(): packed = jnp.dot(one_hot, rows, preferred_element_type=F32).astype(BF)  28.4 us
    ppermute x47, starting transfers between devices, flip(): return lax.ppermute(x, 'tensor', [(i, i ^ mask) for i in range(n_tp)])  20.9 us
    dot_general x3, matrix products, over_tokens(): lax.dot_general(normed1_all, grads, (((0,), (0,)), ((), ())), preferred_e...  19.4 us
  transfers between devices with their start and end apart: 117, of which 31 were waited for; matrix products, arithmetic and copies ran while one was open for 47% of the time, Pallas kernels for 0%

profile of v2, /device:TPU:0, one launch (start us, length us, event | category | flops | bytes accessed | tf_op | source)
XLA Modules:
  0.0 688.2 jit_solution(8454792143851822947)
XLA Ops:
  3.2 5.1 collective-permute-start.8
  65.7 15.7 %collective-permute-done.2 = f32[32,2048]{1,0:T(8,128)S(1)} collective-permute-done((f32[32,2048]{1,0:T(8,128)S(1)}, f32[32,2048]{1,0:T(8,128)S(1)}, u32[]{:S(2)}, u32[]{:S(2)}) %collective-permute-start.2) | collective-permute-done | bytes 262176 | tf_op jit(solution)/shard_map/ppermute | solution.py:95
  84.6 7.2 %collective-permute-done.10 = bf16[32,2048]{1,0:T(8,128)(2,1)S(1)} collective-permute-done((bf16[32,2048]{1,0:T(8,128)(2,1)S(1)}, bf16[32,2048]{1,0:T(8,128)(2,1)S(1)}, u32[]{:S(2)}, u32[]{:S(2)}) %collective-permute-start.10) | collective-permute-done | bytes 131104 | tf_op jit(solution)/shard_map/ppermute | solution.py:92
  94.6 5.0 collective-permute-done.11
  106.7 5.4 collective-permute-done.29
  112.3 6.9 %collective-permute-done.13 = bf16[128,2048]{1,0:T(8,128)(2,1)S(1)} collective-permute-done((bf16[128,2048]{1,0:T(8,128)(2,1)S(1)}, bf16[128,2048]{1,0:T(8,128)(2,1)S(1)}, u32[]{:S(2)}, u32[]{:S(2)}) %collective-permute-start.13) | collective-permute-done | bytes 524320 | tf_op jit(solution)/shard_map/ppermute | solution.py:95
  125.5 10.6 %collective-permute-done.16 = bf16[32,2048]{1,0:T(8,128)(2,1)S(1)} collective-permute-done((bf16[32,2048]{1,0:T(8,128)(2,1)S(1)}, bf16[32,2048]{1,0:T(8,128)(2,1)S(1)}, u32[]{:S(2)}, u32[]{:S(2)}) %collective-permute-start.16) | collective-permute-done | bytes 131104 | tf_op jit(solution)/shard_map/ppermute | solution.py:92
  140.5 13.2 %convolution_convert_fusion.1 = bf16[2560,2048]{1,0:T(8,128)(2,1)} fusion(pred[2560,1024]{1,0:T(32,128)(4,1)S(1)} %bitcast_compare_fusion, bf16[1024,2048]{1,0:T(8,128)(2,1)S(1)} %constant_dynamic-update-slice_fusion.30), kind=kOutput, calls=%fused_computation.3 | convolution fusion | flops 10742661120 | bytes 17301504 | tf_op jit(solution)/shard_map/dot_general | solution.py:263
  154.2 10.0 %fusion.130 = f32[8,320,192]{1,2,0:T(8,128)S(1)} fusion(bf16[8,320,2048]{2,1,0:T(8,128)(2,1)} %bitcast.318, bf16[8,192,2048]{2,1,0:T(8,128)(2,1)} %param.32), kind=kOutput, calls=%fused_computation.454 | convolution fusion | flops 2013265920 | bytes 18743296 | tf_op jit(solution)/shard_map/erd,efd->erf/dot_general | solution.py:275
  183.4 15.2 %convolution_convert_fusion = bf16[2560,2048]{1,0:T(8,128)(2,1)} fusion(pred[2560,1024]{1,0:T(32,128)(4,1)S(1)} %copy-done.16, bf16[1024,2048]{1,0:T(8,128)(2,1)} %constant_dynamic-update-slice_fusion.12), kind=kOutput, calls=%fused_computation.2 | convolution fusion | flops 10742661120 | bytes 17301504 | tf_op jit(solution)/shard_map/dot_general | solution.py:263
  199.3 11.4 %fusion.131 = f32[8,320,192]{1,2,0:T(8,128)} fusion(bf16[8,320,2048]{2,1,0:T(8,128)(2,1)} %bitcast.308, bf16[8,2048,192]{1,2,0:T(8,128)(2,1)} %param.30), kind=kOutput, calls=%fused_computation.455 | convolution fusion | flops 2013265920 | bytes 18743296 | tf_op jit(solution)/shard_map/erd,edf->erf/dot_general | solution.py:278
  211.5 12.6 %fusion.17 = (f32[8,320]{1,0:T(8,128)S(1)}, bf16[8,320,192]{1,2,0:T(8,128)(2,1)}, f32[8,320,192]{1,2,0:T(8,128)}) fusion(f32[8,320,192]{1,2,0:T(8,128)S(1)} %fusion.130, f32[8,320,192]{1,2,0:T(8,128)} %fusion.131, bf16[8,320,2048]{2,1,0:T(8,128)(2,1)} %bitcast.309, bf16[8,2048,192]{1,2,0:T(8,128)(2,1)} %param.31), kind=kOutput, calls=%fused_computation.30 | convolution fusion | flops 2017687040 | bytes 23668736 | tf_op jit(solution)/shard_map/erd,edf->erf/dot_general | solution.py:279
  228.1 5.9 multiply_convert_fusion.1
  234.0 8.6 %fusion.132 = f32[8,320,2048]{2,1,0:T(8,128)} fusion(bf16[8,320,192]{1,2,0:T(8,128)(2,1)S(1)} %get-tuple-element.38, bf16[8,2048,192]{1,2,0:T(8,128)(2,1)S(1)} %bitcast.321), kind=kOutput, calls=%fused_computation.456 | convolution fusion | flops 2013265920 | bytes 28246016 | tf_op jit(solution)/shard_map/erf,edf->erd/dot_general | solution.py:288
  245.1 19.8 %bitcast_convert_fusion.1 = bf16[1024,2048]{1,0:T(8,128)(2,1)} fusion(f32[8,320,2048]{2,1,0:T(8,128)} %fusion.132, bf16[8,320,192]{1,2,0:T(8,128)(2,1)} %get-tuple-element.39, bf16[8,2048,192]{1,2,0:T(8,128)(2,1)} %param.31, pred[8,320,1024]{2,1,0:T(32,128)(4,1)} %iota_compare_fusion.18), kind=kOutput, calls=%fused_computation.17 | convolution fusion | flops 12763267072 | bytes 35061760 | tf_op jit(solution)/shard_map/dot_general | solution.py:268
  276.3 8.3 %collective-permute-done.110 = bf16[128,1024]{1,0:T(8,128)(2,1)S(1)} collective-permute-done((bf16[128,1024]{1,0:T(8,128)(2,1)}, bf16[128,1024]{1,0:T(8,128)(2,1)S(1)}, u32[]{:S(2)}, u32[]{:S(2)}) %collective-permute-start.110) | collective-permute-done | bytes 262176 | tf_op jit(solution)/shard_map/ppermute | solution.py:92
  284.7 16.8 %collective-permute-start.114 = (bf16[128,1024]{1,0:T(8,128)(2,1)}, bf16[128,1024]{1,0:T(8,128)(2,1)S(1)}, u32[]{:S(2)}, u32[]{:S(2)}) collective-permute-start(bf16[128,1024]{1,0:T(8,128)(2,1)} %constant_dynamic-update-slice_fusion.84), channel_id=1, source_target_pairs={{0,20},{4,24},{8,28},{12,0},{16,4},{20,8},{24,12},{28,16},{1,21},{... | collective-permute-start | bytes 786440 | tf_op jit(solution)/shard_map/ppermute | solution.py:92
  301.7 10.3 %collective-permute-done.113 = bf16[128,1024]{1,0:T(8,128)(2,1)S(1)} collective-permute-done((bf16[128,1024]{1,0:T(8,128)(2,1)}, bf16[128,1024]{1,0:T(8,128)(2,1)S(1)}, u32[]{:S(2)}, u32[]{:S(2)}) %collective-permute-start.113) | collective-permute-done | bytes 262176 | tf_op jit(solution)/shard_map/ppermute | solution.py:92
  317.3 9.8 %collective-permute-done.93 = bf16[128,2048]{1,0:T(8,128)(2,1)} collective-permute-done((bf16[128,2048]{1,0:T(8,128)(2,1)S(1)}, bf16[128,2048]{1,0:T(8,128)(2,1)}, u32[]{:S(2)}, u32[]{:S(2)}) %collective-permute-start.93) | collective-permute-done | bytes 524320 | tf_op jit(solution)/shard_map/ppermute | solution.py:95
  327.2 10.0 %collective-permute-start.98 = (bf16[32,2048]{1,0:T(8,128)(2,1)S(1)}, bf16[32,2048]{1,0:T(8,128)(2,1)S(1)}, u32[]{:S(2)}, u32[]{:S(2)}) collective-permute-start(bf16[32,2048]{1,0:T(8,128)(2,1)S(1)} %get-tuple-element.32), channel_id=1, source_target_pairs={{0,24},{4,28},{8,0},{12,4},{16,8},{20,12},{24,16},{28,20},{1,25},{... | collective-permute-start | bytes 393224 | tf_op jit(solution)/shard_map/ppermute | solution.py:92
  341.9 5.9 fusion.207
  347.7 15.4 %bitcast_convert_fusion = bf16[1024,2048]{1,0:T(8,128)(2,1)} fusion(s32[8,1024]{1,0:T(8,128)S(1)} %copy-done.43, bf16[8,320,2048]{2,1,0:T(8,128)(2,1)} %fusion.207), kind=kOutput, calls=%fused_computation.16 | convolution fusion | flops 10742136832 | bytes 14712832 | tf_op jit(solution)/shard_map/dot_general | solution.py:268
  363.2 6.6 fusion.135
  369.8 6.6 fusion.136
  386.6 5.4 collective-permute-done.37
  396.6 7.4 %collective-permute-done.43 = bf16[128,2176]{1,0:T(8,128)(2,1)S(1)} collective-permute-done((bf16[128,2176]{1,0:T(8,128)(2,1)S(1)}, bf16[128,2176]{1,0:T(8,128)(2,1)S(1)}, u32[]{:S(2)}, u32[]{:S(2)}) %collective-permute-start.43) | collective-permute-done | bytes 557088 | tf_op jit(solution)/shard_map/ppermute | solution.py:95
  407.0 7.8 %collective-permute-done.100 = bf16[128,2048]{1,0:T(8,128)(2,1)} collective-permute-done((bf16[128,2048]{1,0:T(8,128)(2,1)S(1)}, bf16[128,2048]{1,0:T(8,128)(2,1)}, u32[]{:S(2)}, u32[]{:S(2)}) %collective-permute-start.100) | collective-permute-done | bytes 524320 | tf_op jit(solution)/shard_map/ppermute | solution.py:95
  417.2 5.3 collective-permute-start.44
  436.6 5.6 collective-permute-start.48
  442.2 12.2 %fusion.134 = f32[8,192,2048]{2,1,0:T(8,128)} fusion(bf16[8,320,192]{1,2,0:T(8,128)(2,1)S(1)} %get-tuple-element.40, bf16[8,320,2048]{2,1,0:T(8,128)(2,1)} %bitcast.319), kind=kOutput, calls=%fused_computation.458 | convolution fusion | flops 2013265920 | bytes 24051712 | tf_op jit(solution)/shard_map/erf,erd->efd/dot_general | solution.py:320
  454.5 4.4 collective-permute-start.53
  465.5 8.6 %collective-permute-done.50 = bf16[128,2176]{1,0:T(8,128)(2,1)S(1)} collective-permute-done((bf16[128,2176]{1,0:T(8,128)(2,1)S(1)}, bf16[128,2176]{1,0:T(8,128)(2,1)S(1)}, u32[]{:S(2)}, u32[]{:S(2)}) %collective-permute-start.50) | collective-permute-done | bytes 557088 | tf_op jit(solution)/shard_map/ppermute | solution.py:95
  505.7 4.8 collective-permute-start.56
  525.2 4.4 collective-permute-done.76
  530.0 11.4 %collective-permute-done.103 = bf16[128,1280]{0,1:T(8,128)(2,1)S(1)} collective-permute-done((bf16[128,1280]{0,1:T(8,128)(2,1)S(1)}, bf16[128,1280]{0,1:T(8,128)(2,1)S(1)}, u32[]{:S(2)}, u32[]{:S(2)}) %collective-permute-start.103) | collective-permute-done | bytes 327712 | tf_op jit(solution)/shard_map/ppermute | solution.py:92
  543.6 13.5 %collective-permute-done.104 = bf16[128,1280]{0,1:T(8,128)(2,1)S(1)} collective-permute-done((bf16[128,1280]{0,1:T(8,128)(2,1)S(1)}, bf16[128,1280]{0,1:T(8,128)(2,1)S(1)}, u32[]{:S(2)}, u32[]{:S(2)}) %collective-permute-start.104) | collective-permute-done | bytes 327712 | tf_op jit(solution)/shard_map/ppermute | solution.py:92
  559.4 7.6 %collective-permute-done.105 = bf16[128,1280]{0,1:T(8,128)(2,1)S(1)} collective-permute-done((bf16[128,1280]{0,1:T(8,128)(2,1)S(1)}, bf16[128,1280]{0,1:T(8,128)(2,1)S(1)}, u32[]{:S(2)}, u32[]{:S(2)}) %collective-permute-start.105) | collective-permute-done | bytes 327712 | tf_op jit(solution)/shard_map/ppermute | solution.py:92
  576.0 12.1 %concatenate.138 = bf16[1024,1280]{0,1:T(8,128)(2,1)} concatenate(bf16[32,1280]{0,1:T(8,128)(2,1)S(1)} %get-tuple-element.149, bf16[32,1280]{0,1:T(8,128)(2,1)} %get-tuple-element.145, bf16[32,1280]{0,1:T(8,128)(2,1)} %get-tuple-element.141, bf16[32,1280]{0,1:T(8,128)(2,1)} %get-tuple-element.137, bf16[32,1280]{0,1:T(8,128)(2,1)S(1)} %get-tuple-element.147, ...), dimensions={0} | concatenate | bytes 5242880 | tf_op jit(solution)/shard_map/concatenate | solution.py:130
  595.4 9.7 %fusion.21 = f32[2048,1024]{1,0:T(8,128)} fusion(bf16[1024,1280]{0,1:T(8,128)(2,1)S(1)} %copy-done.17, bf16[1024,2048]{1,0:T(8,128)(2,1)} %constant_dynamic-update-slice_fusion.70, f32[2048]{0:T(1024)S(1)} %copy-done.57, f32[1024]{0:T(1024)S(1)} %copy-done.75), kind=kOutput, calls=%fused_computation.40 | convolution fusion | flops 4303355904 | bytes 14692352 | tf_op jit(solution)/shard_map/dot_general | solution.py:350
  605.1 4.8 fusion.66
  609.9 4.9 fusion.68
  618.4 12.6 %collective-permute-done.67 = bf16[128,2048]{1,0:T(8,128)(2,1)S(1)} collective-permute-done((bf16[128,2048]{1,0:T(8,128)(2,1)S(1)}, bf16[128,2048]{1,0:T(8,128)(2,1)S(1)}, u32[]{:S(2)}, u32[]{:S(2)}) %collective-permute-start.67) | collective-permute-done | bytes 524320 | tf_op jit(solution)/shard_map/ppermute | solution.py:95
  631.1 8.7 %collective-permute-start.68 = (bf16[32,2048]{1,0:T(8,128)(2,1)S(1)}, bf16[32,2048]{1,0:T(8,128)(2,1)S(1)}, u32[]{:S(2)}, u32[]{:S(2)}) collective-permute-start(bf16[32,2048]{1,0:T(8,128)(2,1)S(1)} %get-tuple-element.113), channel_id=1, source_target_pairs={{0,20},{4,24},{8,28},{12,0},{16,4},{20,8},{24,12},{28,16},{1,21},{... | collective-permute-start | bytes 393224 | tf_op jit(solution)/shard_map/ppermute | solution.py:92
  639.9 5.5 collective-permute-start.70
  645.4 5.6 collective-permute-start.69
  658.5 4.9 collective-permute-start.63
  664.5 10.5 %collective-permute-done.64 = bf16[32,2048]{1,0:T(8,128)(2,1)S(1)} collective-permute-done((bf16[32,2048]{1,0:T(8,128)(2,1)S(1)}, bf16[32,2048]{1,0:T(8,128)(2,1)S(1)}, u32[]{:S(2)}, u32[]{:S(2)}) %collective-permute-start.64) | collective-permute-done | bytes 131104 | tf_op jit(solution)/shard_map/ppermute | solution.py:92
  675.8 6.9 fusion.10
  (653 shorter events, 258.4 us)
Async XLA Ops:
  3.2 45.2 %collective-permute-start.8 = (s32[8,128]{1,0:T(8,128)}, s32[8,128]{1,0:T(8,128)}, u32[]{:S(2)}, u32[]{:S(2)}) collective-permute-start(s32[8,128]{1,0:T(8,128)} %bitcast.16), channel_id=1, source_target_pairs={{0,24},{4,28},{8,0},{12,4},{16,8},{20,12},{24,16},{28,20},{1,25},{... | collective-permute-start | bytes 12296 | tf_op jit(solution)/shard_map/ppermute | solution.py:92
  8.3 38.6 %collective-permute-start.7 = (s32[8,128]{1,0:T(8,128)}, s32[8,128]{1,0:T(8,128)}, u32[]{:S(2)}, u32[]{:S(2)}) collective-permute-start(s32[8,128]{1,0:T(8,128)} %bitcast.16), channel_id=1, source_target_pairs={{0,20},{4,24},{8,28},{12,0},{16,4},{20,8},{24,12},{28,16},{1,21},{... | collective-permute-start | bytes 12296 | tf_op jit(solution)/shard_map/ppermute | solution.py:92
  8.7 35.5 %collective-permute-start.6 = (s32[8,128]{1,0:T(8,128)}, s32[8,128]{1,0:T(8,128)}, u32[]{:S(2)}, u32[]{:S(2)}) collective-permute-start(s32[8,128]{1,0:T(8,128)} %bitcast.16), channel_id=1, source_target_pairs={{0,16},{4,20},{8,24},{12,28},{16,0},{20,4},{24,8},{28,12},{1,17},{... | collective-permute-start | bytes 12296 | tf_op jit(solution)/shard_map/ppermute | solution.py:92
  12.2 30.7 %collective-permute-start.5 = (s32[8,128]{1,0:T(8,128)}, s32[8,128]{1,0:T(8,128)}, u32[]{:S(2)}, u32[]{:S(2)}) collective-permute-start(s32[8,128]{1,0:T(8,128)} %bitcast.16), channel_id=1, source_target_pairs={{0,12},{4,16},{8,20},{12,24},{16,28},{20,0},{24,4},{28,8},{1,13},{... | collective-permute-start | bytes 12296 | tf_op jit(solution)/shard_map/ppermute | solution.py:92
  12.2 23.6 %collective-permute-start.3 = (s32[8,128]{1,0:T(8,128)}, s32[8,128]{1,0:T(8,128)}, u32[]{:S(2)}, u32[]{:S(2)}) collective-permute-start(s32[8,128]{1,0:T(8,128)} %bitcast.16), channel_id=1, source_target_pairs={{0,4},{4,8},{8,12},{12,16},{16,20},{20,24},{24,28},{28,0},{1,5},{5... | collective-permute-start | bytes 12296 | tf_op jit(solution)/shard_map/ppermute | solution.py:92
  42.9 77.3 %collective-permute-start.32 = (bf16[32,2048]{1,0:T(8,128)(2,1)S(1)}, bf16[32,2048]{1,0:T(8,128)(2,1)}, u32[]{:S(2)}, u32[]{:S(2)}) collective-permute-start(bf16[32,2048]{1,0:T(8,128)(2,1)S(1)} %get-tuple-element.62), channel_id=1, source_target_pairs={{0,28},{4,0},{8,4},{12,8},{16,12},{20,16},{24,20},{28,24},{1,29},{... | collective-permute-start | bytes 393224 | tf_op jit(solution)/shard_map/ppermute | solution.py:92
  44.1 68.1 %collective-permute-start.31 = (bf16[32,2048]{1,0:T(8,128)(2,1)S(1)}, bf16[32,2048]{1,0:T(8,128)(2,1)}, u32[]{:S(2)}, u32[]{:S(2)}) collective-permute-start(bf16[32,2048]{1,0:T(8,128)(2,1)S(1)} %get-tuple-element.62), channel_id=1, source_target_pairs={{0,24},{4,28},{8,0},{12,4},{16,8},{20,12},{24,16},{28,20},{1,25},{... | collective-permute-start | bytes 393224 | tf_op jit(solution)/shard_map/ppermute | solution.py:92
  61.4 31.6 %collective-permute-start.26 = (bf16[128,2048]{1,0:T(8,128)(2,1)S(1)}, bf16[128,2048]{1,0:T(8,128)(2,1)S(1)}, u32[]{:S(2)}, u32[]{:S(2)}) collective-permute-start(bf16[128,2048]{1,0:T(8,128)(2,1)S(1)} %pad_maximum_fusion.3), channel_id=1, source_target_pairs={{0,2},{1,3},{2,0},{3,1},{4,6},{5,7},{6,4},{7,5},{8,10},{9,11},{10,... | collective-permute-start | bytes 1572872 | tf_op jit(solution)/shard_map/ppermute | solution.py:95
  112.1 26.7 %collective-permute-start.19 = (bf16[32,2048]{1,0:T(8,128)(2,1)S(1)}, bf16[32,2048]{1,0:T(8,128)(2,1)S(1)}, u32[]{:S(2)}, u32[]{:S(2)}) collective-permute-start(bf16[32,2048]{1,0:T(8,128)(2,1)S(1)} %get-tuple-element.64), channel_id=1, source_target_pairs={{0,28},{4,0},{8,4},{12,8},{16,12},{20,16},{24,20},{28,24},{1,29},{... | collective-permute-start | bytes 393224 | tf_op jit(solution)/shard_map/ppermute | solution.py:92
  112.1 25.9 %collective-permute-start.18 = (bf16[32,2048]{1,0:T(8,128)(2,1)S(1)}, bf16[32,2048]{1,0:T(8,128)(2,1)S(1)}, u32[]{:S(2)}, u32[]{:S(2)}) collective-permute-start(bf16[32,2048]{1,0:T(8,128)(2,1)S(1)} %get-tuple-element.64), channel_id=1, source_target_pairs={{0,24},{4,28},{8,0},{12,4},{16,8},{20,12},{24,16},{28,20},{1,25},{... | collective-permute-start | bytes 393224 | tf_op jit(solution)/shard_map/ppermute | solution.py:92
  139.5 26.9 %collective-permute-start.21 = (bf16[128,2048]{1,0:T(8,128)(2,1)}, bf16[128,2048]{1,0:T(8,128)(2,1)}, u32[]{:S(2)}, u32[]{:S(2)}) collective-permute-start(bf16[128,2048]{1,0:T(8,128)(2,1)} %get-tuple-element.186), channel_id=1, source_target_pairs={{0,1},{1,0},{2,3},{3,2},{4,5},{5,4},{6,7},{7,6},{8,9},{9,8},{10,11... | collective-permute-start | bytes 1572872 | tf_op jit(solution)/shard_map/ppermute | solution.py:95
  170.3 213.9 %collective-permute-start.99 = (bf16[32,2048]{1,0:T(8,128)(2,1)S(1)}, bf16[32,2048]{1,0:T(8,128)(2,1)}, u32[]{:S(2)}, u32[]{:S(2)}) collective-permute-start(bf16[32,2048]{1,0:T(8,128)(2,1)S(1)} %get-tuple-element.32), channel_id=1, source_target_pairs={{0,28},{4,0},{8,4},{12,8},{16,12},{20,16},{24,20},{28,24},{1,29},{... | collective-permute-start | bytes 393224 | tf_op jit(solution)/shard_map/ppermute | solution.py:92
  172.1 101.9 %collective-permute-start.92 = (bf16[32,2048]{1,0:T(8,128)(2,1)S(1)}, bf16[32,2048]{1,0:T(8,128)(2,1)}, u32[]{:S(2)}, u32[]{:S(2)}) collective-permute-start(bf16[32,2048]{1,0:T(8,128)(2,1)S(1)} %get-tuple-element.32), channel_id=1, source_target_pairs={{0,12},{4,16},{8,20},{12,24},{16,28},{20,0},{24,4},{28,8},{1,13},{... | collective-permute-start | bytes 393224 | tf_op jit(solution)/shard_map/ppermute | solution.py:92
  172.1 100.4 %collective-permute-start.91 = (bf16[32,2048]{1,0:T(8,128)(2,1)S(1)}, bf16[32,2048]{1,0:T(8,128)(2,1)}, u32[]{:S(2)}, u32[]{:S(2)}) collective-permute-start(bf16[32,2048]{1,0:T(8,128)(2,1)S(1)} %get-tuple-element.32), channel_id=1, source_target_pairs={{0,8},{4,12},{8,16},{12,20},{16,24},{20,28},{24,0},{28,4},{1,9},{5... | collective-permute-start | bytes 393224 | tf_op jit(solution)/shard_map/ppermute | solution.py:92
  172.3 96.2 %collective-permute-start.90 = (bf16[32,2048]{1,0:T(8,128)(2,1)S(1)}, bf16[32,2048]{1,0:T(8,128)(2,1)}, u32[]{:S(2)}, u32[]{:S(2)}) collective-permute-start(bf16[32,2048]{1,0:T(8,128)(2,1)S(1)} %get-tuple-element.32), channel_id=1, source_target_pairs={{0,4},{4,8},{8,12},{12,16},{16,20},{20,24},{24,28},{28,0},{1,5},{5... | collective-permute-start | bytes 393224 | tf_op jit(solution)/shard_map/ppermute | solution.py:92
  179.3 133.4 %collective-permute-start.116 = (bf16[128,1024]{1,0:T(8,128)(2,1)}, bf16[128,1024]{1,0:T(8,128)(2,1)}, u32[]{:S(2)}, u32[]{:S(2)}) collective-permute-start(bf16[128,1024]{1,0:T(8,128)(2,1)} %constant_dynamic-update-slice_fusion.84), channel_id=1, source_target_pairs={{0,28},{4,0},{8,4},{12,8},{16,12},{20,16},{24,20},{28,24},{1,29},{... | collective-permute-start | bytes 786440 | tf_op jit(solution)/shard_map/ppermute | solution.py:92
  268.4 44.2 %collective-permute-start.115 = (bf16[128,1024]{1,0:T(8,128)(2,1)}, bf16[128,1024]{1,0:T(8,128)(2,1)S(1)}, u32[]{:S(2)}, u32[]{:S(2)}) collective-permute-start(bf16[128,1024]{1,0:T(8,128)(2,1)} %constant_dynamic-update-slice_fusion.84), channel_id=1, source_target_pairs={{0,24},{4,28},{8,0},{12,4},{16,8},{20,12},{24,16},{28,20},{1,25},{... | collective-permute-start | bytes 786440 | tf_op jit(solution)/shard_map/ppermute | solution.py:92
  284.7 27.4 %collective-permute-start.114 = (bf16[128,1024]{1,0:T(8,128)(2,1)}, bf16[128,1024]{1,0:T(8,128)(2,1)S(1)}, u32[]{:S(2)}, u32[]{:S(2)}) collective-permute-start(bf16[128,1024]{1,0:T(8,128)(2,1)} %constant_dynamic-update-slice_fusion.84), channel_id=1, source_target_pairs={{0,20},{4,24},{8,28},{12,0},{16,4},{20,8},{24,12},{28,16},{1,21},{... | collective-permute-start | bytes 786440 | tf_op jit(solution)/shard_map/ppermute | solution.py:92
  312.0 28.0 %collective-permute-start.42 = (bf16[2,128,2176]{2,1,0:T(8,128)(2,1)S(1)}, bf16[2,128,2176]{2,1,0:T(8,128)(2,1)S(1)}, u32[]{:S(2)}, u32[]{:S(2)}) collective-permute-start(bf16[2,128,2176]{2,1,0:T(8,128)(2,1)S(1)} %get-tuple-element.74), channel_id=1, source_target_pairs={{0,1},{1,0},{2,3},{3,2},{4,5},{5,4},{6,7},{7,6},{8,9},{9,8},{10,11... | collective-permute-start | bytes 3342344 | tf_op jit(solution)/shard_map/ppermute | solution.py:95
  312.0 28.0 %collective-permute-start.36 = (bf16[2,128,2176]{2,1,0:T(8,128)(2,1)S(1)}, bf16[2,128,2176]{2,1,0:T(8,128)(2,1)S(1)}, u32[]{:S(2)}, u32[]{:S(2)}) collective-permute-start(bf16[2,128,2176]{2,1,0:T(8,128)(2,1)S(1)} %get-tuple-element.75), channel_id=1, source_target_pairs={{0,1},{1,0},{2,3},{3,2},{4,5},{5,4},{6,7},{7,6},{8,9},{9,8},{10,11... | collective-permute-start | bytes 3342344 | tf_op jit(solution)/shard_map/ppermute | solution.py:95
  312.6 26.5 %collective-permute-start.94 = (bf16[128,2048]{1,0:T(8,128)(2,1)S(1)}, bf16[128,2048]{1,0:T(8,128)(2,1)S(1)}, u32[]{:S(2)}, u32[]{:S(2)}) collective-permute-start(bf16[128,2048]{1,0:T(8,128)(2,1)S(1)} %get-tuple-element.170), channel_id=1, source_target_pairs={{0,1},{1,0},{2,3},{3,2},{4,5},{5,4},{6,7},{7,6},{8,9},{9,8},{10,11... | collective-permute-start | bytes 1572872 | tf_op jit(solution)/shard_map/ppermute | solution.py:95
  327.2 56.4 %collective-permute-start.98 = (bf16[32,2048]{1,0:T(8,128)(2,1)S(1)}, bf16[32,2048]{1,0:T(8,128)(2,1)S(1)}, u32[]{:S(2)}, u32[]{:S(2)}) collective-permute-start(bf16[32,2048]{1,0:T(8,128)(2,1)S(1)} %get-tuple-element.32), channel_id=1, source_target_pairs={{0,24},{4,28},{8,0},{12,4},{16,8},{20,12},{24,16},{28,20},{1,25},{... | collective-permute-start | bytes 393224 | tf_op jit(solution)/shard_map/ppermute | solution.py:92
  339.1 42.9 %collective-permute-start.97 = (bf16[32,2048]{1,0:T(8,128)(2,1)S(1)}, bf16[32,2048]{1,0:T(8,128)(2,1)}, u32[]{:S(2)}, u32[]{:S(2)}) collective-permute-start(bf16[32,2048]{1,0:T(8,128)(2,1)S(1)} %get-tuple-element.32), channel_id=1, source_target_pairs={{0,20},{4,24},{8,28},{12,0},{16,4},{20,8},{24,12},{28,16},{1,21},{... | collective-permute-start | bytes 393224 | tf_op jit(solution)/shard_map/ppermute | solution.py:92
  340.0 39.0 %collective-permute-start.96 = (bf16[32,2048]{1,0:T(8,128)(2,1)S(1)}, bf16[32,2048]{1,0:T(8,128)(2,1)}, u32[]{:S(2)}, u32[]{:S(2)}) collective-permute-start(bf16[32,2048]{1,0:T(8,128)(2,1)S(1)} %get-tuple-element.32), channel_id=1, source_target_pairs={{0,16},{4,20},{8,24},{12,28},{16,0},{20,4},{24,8},{28,12},{1,17},{... | collective-permute-start | bytes 393224 | tf_op jit(solution)/shard_map/ppermute | solution.py:92
  340.0 36.4 %collective-permute-start.95 = (bf16[128,2048]{1,0:T(8,128)(2,1)}, bf16[128,2048]{1,0:T(8,128)(2,1)}, u32[]{:S(2)}, u32[]{:S(2)}) collective-permute-start(bf16[128,2048]{1,0:T(8,128)(2,1)} %collective-permute-done.93), channel_id=1, source_target_pairs={{0,1},{1,0},{2,3},{3,2},{4,5},{5,4},{6,7},{7,6},{8,9},{9,8},{10,11... | collective-permute-start | bytes 1572872 | tf_op jit(solution)/shard_map/ppermute | solution.py:95
  379.0 24.9 %collective-permute-start.43 = (bf16[128,2176]{1,0:T(8,128)(2,1)S(1)}, bf16[128,2176]{1,0:T(8,128)(2,1)S(1)}, u32[]{:S(2)}, u32[]{:S(2)}) collective-permute-start(bf16[128,2176]{1,0:T(8,128)(2,1)S(1)} %slice_bitcast_fusion.8), channel_id=1, source_target_pairs={{0,2},{1,3},{2,0},{3,1},{4,6},{5,7},{6,4},{7,5},{8,10},{9,11},{10,... | collective-permute-start | bytes 1671176 | tf_op jit(solution)/shard_map/ppermute | solution.py:95
  385.9 31.3 %collective-permute-start.101 = (bf16[128,2048]{1,0:T(8,128)(2,1)S(1)}, bf16[128,2048]{1,0:T(8,128)(2,1)S(1)}, u32[]{:S(2)}, u32[]{:S(2)}) collective-permute-start(bf16[128,2048]{1,0:T(8,128)(2,1)S(1)} %get-tuple-element.162), channel_id=1, source_target_pairs={{0,1},{1,0},{2,3},{3,2},{4,5},{5,4},{6,7},{7,6},{8,9},{9,8},{10,11... | collective-permute-start | bytes 1572872 | tf_op jit(solution)/shard_map/ppermute | solution.py:95
  385.9 28.9 %collective-permute-start.100 = (bf16[128,2048]{1,0:T(8,128)(2,1)S(1)}, bf16[128,2048]{1,0:T(8,128)(2,1)}, u32[]{:S(2)}, u32[]{:S(2)}) collective-permute-start(bf16[128,2048]{1,0:T(8,128)(2,1)S(1)} %get-tuple-element.162), channel_id=1, source_target_pairs={{0,2},{1,3},{2,0},{3,1},{4,6},{5,7},{6,4},{7,5},{8,10},{9,11},{10,... | collective-permute-start | bytes 1572872 | tf_op jit(solution)/shard_map/ppermute | solution.py:95
  392.2 30.3 %collective-permute-start.38 = (bf16[32,2176]{1,0:T(8,128)(2,1)S(1)}, bf16[32,2176]{1,0:T(8,128)(2,1)S(1)}, u32[]{:S(2)}, u32[]{:S(2)}) collective-permute-start(bf16[32,2176]{1,0:T(8,128)(2,1)S(1)} %get-tuple-element.88), channel_id=1, source_target_pairs={{0,4},{4,8},{8,12},{12,16},{16,20},{20,24},{24,28},{28,0},{1,5},{5... | collective-permute-start | bytes 417800 | tf_op jit(solution)/shard_map/ppermute | solution.py:92
  393.7 28.7 %collective-permute-start.41 = (bf16[32,2176]{1,0:T(8,128)(2,1)S(1)}, bf16[32,2176]{1,0:T(8,128)(2,1)S(1)}, u32[]{:S(2)}, u32[]{:S(2)}) collective-permute-start(bf16[32,2176]{1,0:T(8,128)(2,1)S(1)} %get-tuple-element.89), channel_id=1, source_target_pairs={{0,16},{4,20},{8,24},{12,28},{16,0},{20,4},{24,8},{28,12},{1,17},{... | collective-permute-start | bytes 417800 | tf_op jit(solution)/shard_map/ppermute | solution.py:92
  403.9 21.3 %collective-permute-start.40 = (bf16[32,2176]{1,0:T(8,128)(2,1)S(1)}, bf16[32,2176]{1,0:T(8,128)(2,1)S(1)}, u32[]{:S(2)}, u32[]{:S(2)}) collective-permute-start(bf16[32,2176]{1,0:T(8,128)(2,1)S(1)} %get-tuple-element.90), channel_id=1, source_target_pairs={{0,12},{4,16},{8,20},{12,24},{16,28},{20,0},{24,4},{28,8},{1,13},{... | collective-permute-start | bytes 417800 | tf_op jit(solution)/shard_map/ppermute | solution.py:92
  425.2 34.6 %collective-permute-start.102 = (bf16[128,2048]{1,0:T(8,128)(2,1)}, bf16[128,2048]{1,0:T(8,128)(2,1)}, u32[]{:S(2)}, u32[]{:S(2)}) collective-permute-start(bf16[128,2048]{1,0:T(8,128)(2,1)} %collective-permute-done.100), channel_id=1, source_target_pairs={{0,1},{1,0},{2,3},{3,2},{4,5},{5,4},{6,7},{7,6},{8,9},{9,8},{10,11... | collective-permute-start | bytes 1572872 | tf_op jit(solution)/shard_map/ppermute | solution.py:95
  433.7 65.0 %collective-permute-start.54 = (bf16[32,2176]{1,0:T(8,128)(2,1)S(1)}, bf16[32,2176]{1,0:T(8,128)(2,1)S(1)}, u32[]{:S(2)}, u32[]{:S(2)}) collective-permute-start(bf16[32,2176]{1,0:T(8,128)(2,1)S(1)} %concatenate.123), channel_id=1, source_target_pairs={{0,20},{4,24},{8,28},{12,0},{16,4},{20,8},{24,12},{28,16},{1,21},{... | collective-permute-start | bytes 417800 | tf_op jit(solution)/shard_map/ppermute | solution.py:92
  434.6 19.9 %collective-permute-start.49 = (bf16[32,2176]{1,0:T(8,128)(2,1)S(1)}, bf16[32,2176]{1,0:T(8,128)(2,1)S(1)}, u32[]{:S(2)}, u32[]{:S(2)}) collective-permute-start(bf16[32,2176]{1,0:T(8,128)(2,1)S(1)} %concatenate.123), channel_id=1, source_target_pairs={{0,12},{4,16},{8,20},{12,24},{16,28},{20,0},{24,4},{28,8},{1,13},{... | collective-permute-start | bytes 417800 | tf_op jit(solution)/shard_map/ppermute | solution.py:92
  436.6 22.3 %collective-permute-start.48 = (bf16[32,2176]{1,0:T(8,128)(2,1)S(1)}, bf16[32,2176]{1,0:T(8,128)(2,1)S(1)}, u32[]{:S(2)}, u32[]{:S(2)}) collective-permute-start(bf16[32,2176]{1,0:T(8,128)(2,1)S(1)} %concatenate.123), channel_id=1, source_target_pairs={{0,8},{4,12},{8,16},{12,20},{16,24},{20,28},{24,0},{28,4},{1,9},{5... | collective-permute-start | bytes 417800 | tf_op jit(solution)/shard_map/ppermute | solution.py:92
  454.5 41.5 %collective-permute-start.53 = (bf16[32,2176]{1,0:T(8,128)(2,1)S(1)}, bf16[32,2176]{1,0:T(8,128)(2,1)}, u32[]{:S(2)}, u32[]{:S(2)}) collective-permute-start(bf16[32,2176]{1,0:T(8,128)(2,1)S(1)} %concatenate.123), channel_id=1, source_target_pairs={{0,16},{4,20},{8,24},{12,28},{16,0},{20,4},{24,8},{28,12},{1,17},{... | collective-permute-start | bytes 417800 | tf_op jit(solution)/shard_map/ppermute | solution.py:92
  510.5 64.2 %collective-permute-start.109 = (bf16[128,1280]{0,1:T(8,128)(2,1)S(1)}, bf16[128,1280]{0,1:T(8,128)(2,1)S(1)}, u32[]{:S(2)}, u32[]{:S(2)}) collective-permute-start(bf16[128,1280]{0,1:T(8,128)(2,1)S(1)} %pad_maximum_fusion.6), channel_id=1, source_target_pairs={{0,28},{4,0},{8,4},{12,8},{16,12},{20,16},{24,20},{28,24},{1,29},{... | collective-permute-start | bytes 983048 | tf_op jit(solution)/shard_map/ppermute | solution.py:92
  510.6 61.7 %collective-permute-start.108 = (bf16[128,1280]{0,1:T(8,128)(2,1)S(1)}, bf16[128,1280]{0,1:T(8,128)(2,1)S(1)}, u32[]{:S(2)}, u32[]{:S(2)}) collective-permute-start(bf16[128,1280]{0,1:T(8,128)(2,1)S(1)} %pad_maximum_fusion.6), channel_id=1, source_target_pairs={{0,24},{4,28},{8,0},{12,4},{16,8},{20,12},{24,16},{28,20},{1,25},{... | collective-permute-start | bytes 983048 | tf_op jit(solution)/shard_map/ppermute | solution.py:92
  511.9 58.7 %collective-permute-start.107 = (bf16[128,1280]{0,1:T(8,128)(2,1)S(1)}, bf16[128,1280]{0,1:T(8,128)(2,1)S(1)}, u32[]{:S(2)}, u32[]{:S(2)}) collective-permute-start(bf16[128,1280]{0,1:T(8,128)(2,1)S(1)} %pad_maximum_fusion.6), channel_id=1, source_target_pairs={{0,20},{4,24},{8,28},{12,0},{16,4},{20,8},{24,12},{28,16},{1,21},{... | collective-permute-start | bytes 983048 | tf_op jit(solution)/shard_map/ppermute | solution.py:92
  525.2 43.1 %collective-permute-start.106 = (bf16[128,1280]{0,1:T(8,128)(2,1)S(1)}, bf16[128,1280]{0,1:T(8,128)(2,1)S(1)}, u32[]{:S(2)}, u32[]{:S(2)}) collective-permute-start(bf16[128,1280]{0,1:T(8,128)(2,1)S(1)} %pad_maximum_fusion.6), channel_id=1, source_target_pairs={{0,16},{4,20},{8,24},{12,28},{16,0},{20,4},{24,8},{28,12},{1,17},{... | collective-permute-start | bytes 983048 | tf_op jit(solution)/shard_map/ppermute | solution.py:92
  566.9 23.3 %collective-permute-start.58 = (bf16[128,2176]{1,0:T(8,128)(2,1)}, bf16[128,2176]{1,0:T(8,128)(2,1)}, u32[]{:S(2)}, u32[]{:S(2)}) collective-permute-start(bf16[128,2176]{1,0:T(8,128)(2,1)} %get-tuple-element.154), channel_id=1, source_target_pairs={{0,1},{1,0},{2,3},{3,2},{4,5},{5,4},{6,7},{7,6},{8,9},{9,8},{10,11... | collective-permute-start | bytes 1671176 | tf_op jit(solution)/shard_map/ppermute | solution.py:95
  568.3 19.9 %collective-permute-start.57 = (bf16[128,2176]{1,0:T(8,128)(2,1)}, bf16[128,2176]{1,0:T(8,128)(2,1)}, u32[]{:S(2)}, u32[]{:S(2)}) collective-permute-start(bf16[128,2176]{1,0:T(8,128)(2,1)} %get-tuple-element.154), channel_id=1, source_target_pairs={{0,2},{1,3},{2,0},{3,1},{4,6},{5,7},{6,4},{7,5},{8,10},{9,11},{10,... | collective-permute-start | bytes 1671176 | tf_op jit(solution)/shard_map/ppermute | solution.py:95
  570.7 46.5 %collective-permute-start.79 = (bf16[32,2048]{1,0:T(8,128)(2,1)S(1)}, bf16[32,2048]{1,0:T(8,128)(2,1)S(1)}, u32[]{:S(2)}, u32[]{:S(2)}) collective-permute-start(bf16[32,2048]{1,0:T(8,128)(2,1)S(1)} %fusion.55), channel_id=1, source_target_pairs={{0,1},{1,0},{2,3},{3,2},{4,5},{5,4},{6,7},{7,6},{8,9},{9,8},{10,11... | collective-permute-start | bytes 393224 | tf_op jit(solution)/shard_map/ppermute | solution.py:95
  572.3 42.5 %collective-permute-start.77 = (bf16[32,2048]{1,0:T(8,128)(2,1)S(1)}, bf16[32,2048]{1,0:T(8,128)(2,1)S(1)}, u32[]{:S(2)}, u32[]{:S(2)}) collective-permute-start(bf16[32,2048]{1,0:T(8,128)(2,1)S(1)} %fusion.55), channel_id=1, source_target_pairs={{0,2},{1,3},{2,0},{3,1},{4,6},{5,7},{6,4},{7,5},{8,10},{9,11},{10,... | collective-permute-start | bytes 393224 | tf_op jit(solution)/shard_map/ppermute | solution.py:95
  594.7 20.5 %collective-permute-start.60 = (bf16[2,128,2048]{2,1,0:T(8,128)(2,1)S(1)}, bf16[2,128,2048]{2,1,0:T(8,128)(2,1)S(1)}, u32[]{:S(2)}, u32[]{:S(2)}) collective-permute-start(bf16[2,128,2048]{2,1,0:T(8,128)(2,1)S(1)} %get-tuple-element.78), channel_id=1, source_target_pairs={{0,1},{1,0},{2,3},{3,2},{4,5},{5,4},{6,7},{7,6},{8,9},{9,8},{10,11... | collective-permute-start | bytes 3145736 | tf_op jit(solution)/shard_map/ppermute | solution.py:95
  595.3 19.9 %collective-permute-start.66 = (bf16[2,128,2048]{2,1,0:T(8,128)(2,1)S(1)}, bf16[2,128,2048]{2,1,0:T(8,128)(2,1)S(1)}, u32[]{:S(2)}, u32[]{:S(2)}) collective-permute-start(bf16[2,128,2048]{2,1,0:T(8,128)(2,1)S(1)} %get-tuple-element.79), channel_id=1, source_target_pairs={{0,1},{1,0},{2,3},{3,2},{4,5},{5,4},{6,7},{7,6},{8,9},{9,8},{10,11... | collective-permute-start | bytes 3145736 | tf_op jit(solution)/shard_map/ppermute | solution.py:95
  617.3 33.7 %collective-permute-start.61 = (bf16[128,2048]{1,0:T(8,128)(2,1)S(1)}, bf16[128,2048]{1,0:T(8,128)(2,1)S(1)}, u32[]{:S(2)}, u32[]{:S(2)}) collective-permute-start(bf16[128,2048]{1,0:T(8,128)(2,1)S(1)} %slice_bitcast_fusion.14), channel_id=1, source_target_pairs={{0,2},{1,3},{2,0},{3,1},{4,6},{5,7},{6,4},{7,5},{8,10},{9,11},{10,... | collective-permute-start | bytes 1572872 | tf_op jit(solution)/shard_map/ppermute | solution.py:95
  631.1 24.4 %collective-permute-start.68 = (bf16[32,2048]{1,0:T(8,128)(2,1)S(1)}, bf16[32,2048]{1,0:T(8,128)(2,1)S(1)}, u32[]{:S(2)}, u32[]{:S(2)}) collective-permute-start(bf16[32,2048]{1,0:T(8,128)(2,1)S(1)} %get-tuple-element.113), channel_id=1, source_target_pairs={{0,20},{4,24},{8,28},{12,0},{16,4},{20,8},{24,12},{28,16},{1,21},{... | collective-permute-start | bytes 393224 | tf_op jit(solution)/shard_map/ppermute | solution.py:92
  (164 other events, 2928.6 us)
